TPU v7x, 512 devices: a whole 4x8x8 slice. The times are simulated.
512 devices in a mesh: trans: 64 (over z, x, y_hi), los: 8 (over y_lo, core).
Axes of the slice: x: 4, y: 8 (y_hi: 2, y_lo: 4; y = y_hi * 4 + y_lo), z: 8, core: 2. Of those that a mesh axis runs over, the one named last changes fastest.
Arguments:
- density: bfloat16 [8, 2048, 2048], P('los', 'trans'), may hold values from -6 to 6
- row_pos: float32 [8, 2048], replicated, may hold values from 0 to 2048
- col_pos: float32 [8, 2048], replicated, may hold values from 0 to 2048
- plane_of_slot: int32 [8], replicated, may hold values from 0 to 7, each once
- plane_bin: int32 [8], replicated, may hold values from 0 to 3, as said below
- efficiency: float32 [4, 8], replicated, may hold values from 0.3 to 3
Outputs:
- shear: float32 [2, 4, 2048, 2048], P(None, None, ('trans', 'los'))
Inputs may be any that keep to these rules, and one draw needn't show every extreme that they name: `plane_bin`: some plane has bin 0 and some plane has bin 4 - 1.
All inputs are finite; a program needn't handle non-finite values.
Results may differ from a plain program's by a relative error of at most 0.006.
Values may be sent and summed in bfloat16 or wider, within the bound.
No kernel may reach another device: no remote copies, remote signals or barrier semaphores. Data moves between devices by JAX's collectives and lax.ppermute only.
A program may use at most 64 MiB of HBM per device.

v0:
```python
import math

import jax
import jax.numpy as jnp
from jax import lax
from jax.sharding import PartitionSpec as P


def hat_block(positions, mesh_cells):
    cells = jnp.arange(mesh_cells, dtype=jnp.int32).astype(jnp.float32)
    offset = positions[:, None] - cells[None, :] + 0.5 * mesh_cells
    folded = jnp.mod(offset, 1.0 * mesh_cells) - 0.5 * mesh_cells
    return jnp.maximum(1.0 - jnp.abs(folded), 0.0).astype(jnp.bfloat16)


def trig_pair(rows_n, cols_n, modulus, sign_value):
    product_index = (
        jnp.arange(rows_n, dtype=jnp.int32)[:, None]
        * jnp.arange(cols_n, dtype=jnp.int32)[None, :]
        % modulus
    )
    angle = product_index.astype(jnp.float32) * (2.0 * math.pi / modulus)
    return (jnp.cos(angle), sign_value * jnp.sin(angle))


def fourier(real_part, imag_part, inverse):
    length = real_part.shape[-1]
    factor_one = 16
    second = length // factor_one
    sign_value = 1.0 if inverse else -1.0
    lead_shape = real_part.shape[:-1]
    highest = lax.Precision.HIGHEST
    cos_one, sin_one = trig_pair(factor_one, factor_one, factor_one, sign_value)
    real_grid = real_part.reshape(lead_shape + (factor_one, second))
    imag_grid = imag_part.reshape(lead_shape + (factor_one, second))

    def first_pass(table, values):
        return jnp.einsum("kn,...nm->...km", table, values, precision=highest)

    section_real = first_pass(cos_one, real_grid) - first_pass(sin_one, imag_grid)
    section_imag = first_pass(cos_one, imag_grid) + first_pass(sin_one, real_grid)
    cos_twid, sin_twid = trig_pair(factor_one, second, length, sign_value)
    turned_real = section_real * cos_twid - section_imag * sin_twid
    turned_imag = section_real * sin_twid + section_imag * cos_twid
    cos_two, sin_two = trig_pair(second, second, second, sign_value)

    def second_pass(values, table):
        return jnp.einsum("...km,mj->...kj", values, table, precision=highest)

    out_real = second_pass(turned_real, cos_two) - second_pass(turned_imag, sin_two)
    out_imag = second_pass(turned_real, sin_two) + second_pass(turned_imag, cos_two)
    out_real = jnp.swapaxes(out_real, -1, -2).reshape(lead_shape + (length,))
    out_imag = jnp.swapaxes(out_imag, -1, -2).reshape(lead_shape + (length,))
    scale = 1.0 / length if inverse else 1.0
    return (out_real * scale, out_imag * scale)


def wave_numbers(index_all, length):
    return jnp.where(index_all < length // 2, index_all, index_all - length).astype(jnp.float32)


def body(density, row_pos, col_pos, plane_of_slot, plane_bin, efficiency):
    count_trans = lax.axis_size("trans")
    count_los = lax.axis_size("los")
    per_device = density.shape[0]
    mesh_cells = density.shape[2]
    grid_cells = row_pos.shape[1]
    planes_total = row_pos.shape[0]
    bins_total = efficiency.shape[0]
    width_cols = grid_cells // (count_trans * count_los)
    block_rows = min(512, grid_cells)
    slots = jnp.arange(planes_total, dtype=jnp.int32)
    bin_index = jnp.arange(bins_total, dtype=jnp.int32)
    by_columns = lax.all_to_all(density, "trans", split_axis=2, concat_axis=1, tiled=True)
    local_slot = 0
    slot_now = lax.axis_index("los") * per_device + local_slot
    plane_id = jnp.sum(jnp.where(slots == slot_now, plane_of_slot, 0))
    chosen = slots == plane_id
    plane_eff = jnp.sum(jnp.where(chosen[None, :], efficiency, 0.0), axis=1)
    first_bin = jnp.sum(jnp.where(chosen, plane_bin, 0))
    weight_list = [plane_eff * (bin_index >= first_bin).astype(jnp.float32)]
    rows_here = jnp.sum(jnp.where(chosen[:, None], row_pos, 0.0), axis=0)
    cols_here = jnp.sum(jnp.where(chosen[:, None], col_pos, 0.0), axis=0)
    pieces = []
    for begin in range(0, grid_cells, block_rows):
        row_block = hat_block(rows_here[begin : begin + block_rows], mesh_cells)
        pieces.append(
            lax.dot_general(
                by_columns[local_slot],
                row_block,
                (((0,), (1,)), ((), ())),
                preferred_element_type=jnp.float32,
            )
        )
    resampled = [jnp.concatenate(pieces, axis=1).astype(jnp.bfloat16)]
    col_tables = [hat_block(cols_here, mesh_cells)]
    half_columns = jnp.stack(resampled)
    exchanged = lax.all_to_all(half_columns, "trans", split_axis=2, concat_axis=1, tiled=True)
    local_slot = 0
    rows_map = lax.dot_general(
        exchanged[local_slot],
        col_tables[local_slot],
        (((0,), (1,)), ((), ())),
        preferred_element_type=jnp.float32,
    )
    plane_term = weight_list[local_slot][None, :, None] * rows_map[:, None, :]
    term_real, term_imag = fourier(plane_term, jnp.zeros_like(plane_term), False)
    summed_real, summed_imag = (
        lax.psum_scatter(term_real, "los", scatter_dimension=2, tiled=True),
        lax.psum_scatter(term_imag, "los", scatter_dimension=2, tiled=True),
    )
    arrived = lax.all_to_all(
        jnp.stack([summed_real, summed_imag]), "trans", split_axis=3, concat_axis=1, tiled=True
    )
    columns_local = arrived.transpose(0, 2, 3, 1)
    col_index = (
        lax.axis_index("los") * (grid_cells // count_los)
        + lax.axis_index("trans") * width_cols
        + jnp.arange(width_cols, dtype=jnp.int32)
    )
    freq_real, freq_imag = fourier(columns_local[0], columns_local[1], False)
    wave_rows = wave_numbers(jnp.arange(grid_cells, dtype=jnp.int32), grid_cells)[None, :]
    wave_cols = wave_numbers(col_index, grid_cells)[:, None]
    square_sum = jnp.maximum(wave_rows * wave_rows + wave_cols * wave_cols, 1.0)
    first_factor = (wave_rows * wave_rows - wave_cols * wave_cols) / square_sum
    second_factor = 2.0 * wave_rows * wave_cols / square_sum
    kernel_real = first_factor * freq_real - second_factor * freq_imag
    kernel_imag = first_factor * freq_imag + second_factor * freq_real
    back_real, back_imag = fourier(kernel_real, kernel_imag, True)
    returned = jnp.stack([back_real, back_imag]).transpose(0, 3, 1, 2)
    rows_local = lax.all_to_all(
        lax.all_to_all(returned, "trans", split_axis=1, concat_axis=3, tiled=True),
        "los",
        split_axis=1,
        concat_axis=3,
        tiled=True,
    )
    final_real, final_imag = fourier(rows_local[0], rows_local[1], True)
    return jnp.stack([final_real, final_imag]).transpose(0, 2, 1, 3)


def solution(mesh):
    placed = (P("los", "trans", None), P(), P(), P(), P(), P())
    return jax.shard_map(
        body,
        mesh=mesh,
        in_specs=placed,
        out_specs=P(None, None, ("trans", "los"), None),
        check_vma=False,
    )
```

profile of v0, /device:TPU:1, one launch (start us, length us, event | category | flops | bytes accessed | tf_op | source)
XLA Modules:
  0.0 373.0 jit_solution(723712246970440982)
XLA Ops:
  6.5 2.1 copy.54
  9.1 11.5 %reduce = bf16[2048,32]{1,0:T(8,128)(2,1)S(1)} reduce(bf16[2048,1,32]{2,1,0:T(2,128)(2,1)S(1)} %bitcast.212, bf16[]{:T(256)} %broadcast.787), dimensions={1}, to_apply=%bitcast.179.reduce_sub_computation | reduce | bytes 262146
  20.6 1.1 reshape.412
  21.7 19.8 %all-to-all-start = ((bf16[64,2,512]{2,1,0:T(2,128)(2,1)}), bf16[64,2,512]{2,1,0:T(2,128)(2,1)S(1)}, u32[]{:S(2)}, u32[]{:S(2)}) async-start(bf16[64,2,512]{2,1,0:T(2,128)(2,1)} %reshape.412), calls=%async_computation | async-start | bytes 262144 | tf_op jit(solution)/shard_map/all_to_all | solution.py:74
  42.8 0.7 fusion.238
  43.5 0.7 iota_compare_fusion
  44.5 10.6 %all-to-all-done = bf16[64,2,512]{2,1,0:T(2,128)(2,1)S(1)} async-done(((bf16[64,2,512]{2,1,0:T(2,128)(2,1)}), bf16[64,2,512]{2,1,0:T(2,128)(2,1)S(1)}, u32[]{:S(2)}, u32[]{:S(2)}) %all-to-all-start) | async-done | bytes 131104 | tf_op jit(solution)/shard_map/all_to_all | solution.py:74
  55.1 0.7 reshape.413
  56.7 1.1 copy.56
  58.3 3.3 fusion.96
  61.7 3.3 fusion.99
  65.0 3.3 fusion.102
  68.3 3.3 fusion.105
  71.7 0.7 copy.57
  72.4 12.7 %reduce.1 = bf16[2048,32]{1,0:T(8,128)(2,1)} reduce(bf16[2048,1,32]{2,1,0:T(2,128)(2,1)S(1)} %bitcast.213, bf16[]{:T(256)} %broadcast.787), dimensions={1}, to_apply=%bitcast.181.reduce_sub_computation | reduce | bytes 262146
  85.0 2.1 reshape.414
  87.2 4.6 %all-to-all-start.1 = ((bf16[64,2,512]{2,1,0:T(2,128)(2,1)}), bf16[64,2,512]{2,1,0:T(2,128)(2,1)S(1)}, u32[]{:S(2)}, u32[]{:S(2)}) async-start(bf16[64,2,512]{2,1,0:T(2,128)(2,1)} %reshape.414), calls=%async_computation.1 | async-start | bytes 262144 | tf_op jit(solution)/shard_map/all_to_all | solution.py:98
  91.9 1.4 select_reduce_fusion.3
  93.3 0.7 compare_select_fusion.2
  94.0 11.4 %all-to-all-done.1 = bf16[64,2,512]{2,1,0:T(2,128)(2,1)S(1)} async-done(((bf16[64,2,512]{2,1,0:T(2,128)(2,1)}), bf16[64,2,512]{2,1,0:T(2,128)(2,1)S(1)}, u32[]{:S(2)}, u32[]{:S(2)}) %all-to-all-start.1) | async-done | bytes 131104 | tf_op jit(solution)/shard_map/all_to_all | solution.py:98
  105.3 0.7 reshape.415
  106.0 0.7 copy.58
  107.1 1.1 copy.59
  108.8 12.4 %fusion.8 = f32[32,16,128]{2,0,1:T(8,128)S(1)} fusion(bf16[2048,32,1]{0,1,2:T(8,128)(2,1)S(1)} %reshape.400, f32[2048]{0:T(1024)S(1)} %iota_convert_fusion, f32[16,128]{1,0:T(8,128)S(1)} %bitcast.221), kind=kOutput, calls=%fused_computation.10 | convolution fusion | flops 322961408 | bytes 409600 | tf_op jit(solution)/shard_map/dot_general | solution.py:100
  121.3 1.1 fusion.57
  122.4 1.1 fusion.63
  123.5 1.2 fusion.117
  124.8 1.2 fusion.67
  126.0 3.2 copy.61
  129.3 1.2 fusion.116
  130.6 1.2 fusion.66
  131.8 3.4 copy.62
  135.3 43.1 %reduce-scatter.3.cloned.1.call-done = f32[32,4,256]{0,2,1:T(8,128)} async-done(((f32[32,4,2048]{0,2,1:T(8,128)}), f32[32,4,256]{0,2,1:T(8,128)}) %reduce-scatter.3.cloned.1.call-update) | async-done | bytes 131088 | tf_op jit(solution)/shard_map/reduce_scatter | solution.py:109
  178.4 59.6 %reduce-scatter.5.cloned.1.call-done = f32[32,4,256]{0,2,1:T(8,128)} async-done(((f32[32,4,2048]{0,2,1:T(8,128)}), f32[32,4,256]{0,2,1:T(8,128)}) %reduce-scatter.5.cloned.1.call-update) | async-done | bytes 131088 | tf_op jit(solution)/shard_map/reduce_scatter | solution.py:110
  238.0 1.3 pad_maximum_fusion
  240.0 1.4 reshape.416
  241.3 14.8 %all-to-all-start.2 = ((f32[64,1,1024]{2,1,0:T(1,128)}), f32[64,1,1024]{2,1,0:T(1,128)S(1)}, u32[]{:S(2)}, u32[]{:S(2)}) async-start(f32[64,1,1024]{2,1,0:T(1,128)} %reshape.416), calls=%async_computation.4 | async-start | bytes 524288 | tf_op jit(solution)/shard_map/all_to_all | solution.py:112
  256.3 13.9 %all-to-all-done.2 = f32[64,1,1024]{2,1,0:T(1,128)S(1)} async-done(((f32[64,1,1024]{2,1,0:T(1,128)}), f32[64,1,1024]{2,1,0:T(1,128)S(1)}, u32[]{:S(2)}, u32[]{:S(2)}) %all-to-all-start.2) | async-done | bytes 262176 | tf_op jit(solution)/shard_map/all_to_all | solution.py:112
  270.7 1.3 reduce.2
  283.5 5.9 %copy.70 = f32[2,2048,4,4]{3,2,0,1:T(4,128)} copy(f32[2,2048,4,4]{1,3,2,0:T(4,128)S(1)} %maximum_bitcast_fusion) | data formatting | bytes 524288 | tf_op jit(solution)/shard_map/transpose | solution.py:130
  289.4 11.5 %reshape.418 = f32[64,1,1024]{2,1,0:T(1,128)S(1)} reshape(f32[2048,2,4,4]{3,2,1,0:T(4,128)} %bitcast.202) | data formatting | bytes 524288
  300.9 21.5 %all_to_all.81 = f32[64,1,1024]{2,1,0:T(1,128)S(1)} all-to-all(f32[64,1,1024]{2,1,0:T(1,128)S(1)} %reshape.418), channel_id=1, replica_groups=mesh['trans'=64,'los'=8] {'trans'}, dimensions={0} | all-to-all | bytes 524288 | tf_op jit(solution)/shard_map/all_to_all | solution.py:132
  322.4 1.3 reduce.3
  323.7 12.3 %reshape.419 = f32[2048,2,4,4]{3,2,1,0:T(4,128)} reshape(f32[64,1024]{1,0:T(8,128)S(1)} %reduce.3) | data formatting | bytes 524288
  335.9 7.6 %copy.86 = f32[2,64,32,4,4]{2,1,4,3,0:T(8,128)S(1)} copy(f32[2,64,32,4,4]{4,3,0,2,1:T(4,128)} %bitcast.203) | data formatting | bytes 524288 | tf_op jit(solution)/shard_map/all_to_all | solution.py:132
  343.5 0.7 copy.72
  344.5 15.1 %all_to_all.82 = f32[2,32,4,256]{3,2,0,1:T(4,128)S(1)} all-to-all(f32[2,32,4,256]{3,2,0,1:T(4,128)S(1)} %copy.73), channel_id=1, replica_groups=mesh['trans'=64,'los'=8] {'los'}, dimensions={1} | all-to-all | bytes 524288 | tf_op jit(solution)/shard_map/all_to_all | solution.py:131
  365.1 0.9 copy.79
  (88 shorter events, 23.0 us)
Async XLA Ops:
  6.5 36.3 %copy-start.3 = (s32[8]{0:T(128)S(1)}, s32[8]{0:T(128)}, u32[]{:S(2)}) copy-start(s32[8]{0:T(128)} %param.9) | copy-start | bytes 100
  6.5 37.7 %copy-start = (f32[8,2048]{1,0:T(8,128)S(1)}, f32[8,2048]{1,0:T(8,128)}, u32[]{:S(2)}) copy-start(f32[8,2048]{1,0:T(8,128)} %param.8) | copy-start | bytes 196612
  6.5 37.7 %copy-start.1 = (f32[8,2048]{1,0:T(8,128)S(1)}, f32[8,2048]{1,0:T(8,128)}, u32[]{:S(2)}) copy-start(f32[8,2048]{1,0:T(8,128)} %param.7) | copy-start | bytes 196612
  6.5 37.8 %copy-start.2 = (f32[4,8]{1,0:T(4,128)S(1)}, f32[4,8]{1,0:T(4,128)}, u32[]{:S(2)}) copy-start(f32[4,8]{1,0:T(4,128)} %param.11) | copy-start | bytes 388
  21.7 33.4 %all-to-all-start = ((bf16[64,2,512]{2,1,0:T(2,128)(2,1)}), bf16[64,2,512]{2,1,0:T(2,128)(2,1)S(1)}, u32[]{:S(2)}, u32[]{:S(2)}) async-start(bf16[64,2,512]{2,1,0:T(2,128)(2,1)} %reshape.412), calls=%async_computation | async-start | bytes 262144 | tf_op jit(solution)/shard_map/all_to_all | solution.py:74
  68.3 23.6 %copy-start.4 = (s32[8]{0:T(128)S(1)}, s32[8]{0:T(128)}, u32[]{:S(2)}) copy-start(s32[8]{0:T(128)} %param.10) | copy-start | bytes 100
  87.2 18.1 %all-to-all-start.1 = ((bf16[64,2,512]{2,1,0:T(2,128)(2,1)}), bf16[64,2,512]{2,1,0:T(2,128)(2,1)S(1)}, u32[]{:S(2)}, u32[]{:S(2)}) async-start(bf16[64,2,512]{2,1,0:T(2,128)(2,1)} %reshape.414), calls=%async_computation.1 | async-start | bytes 262144 | tf_op jit(solution)/shard_map/all_to_all | solution.py:98
  91.8 86.6 %reduce-scatter.3.cloned.1.call-start = ((), (), s32[]{:S(2)}) async-start(), calls=%async_computation.7 | async-start | bytes 4718592 | tf_op jit(solution)/shard_map/reduce_scatter | solution.py:109
  129.3 108.7 %reduce-scatter.5.cloned.1.call-start = ((), (), s32[]{:S(2)}) async-start(), calls=%async_computation.8 | async-start | bytes 4718592 | tf_op jit(solution)/shard_map/reduce_scatter | solution.py:110
  241.3 28.9 %all-to-all-start.2 = ((f32[64,1,1024]{2,1,0:T(1,128)}), f32[64,1,1024]{2,1,0:T(1,128)S(1)}, u32[]{:S(2)}, u32[]{:S(2)}) async-start(f32[64,1,1024]{2,1,0:T(1,128)} %reshape.416), calls=%async_computation.4 | async-start | bytes 524288 | tf_op jit(solution)/shard_map/all_to_all | solution.py:112
Sparse Core Ops, SparseCore 0:
  129.4 48.9 reduce-scatter.2
  181.2 56.7 reduce-scatter.4
where the time goes:
time: 379 us; the launch traced here: 373 us
  waiting for transfers between devices  139 us (37%)
  local copies, waits for them, and re-layouts  68.3 us (18%)
  matrix products  43.9 us (12%)
  starting transfers between devices  39.3 us (10%)
  blocking collectives  36.6 us (10%)
  other arithmetic  32 us (8%)
  between operations  14.4 us (4%)
    reduce_scatter x1, waiting for transfers between devices, body(): lax.psum_scatter(term_imag, 'los', scatter_dimension=2, tiled=True)  59.6 us
    reduce_scatter x1, waiting for transfers between devices, body(): lax.psum_scatter(term_real, 'los', scatter_dimension=2, tiled=True)  43.1 us
    unnamed x20, local copies, waits for them, and re-layouts  32.8 us
    unnamed x2, other arithmetic  24.1 us
    all_to_all x1, blocking collectives, body(): lax.all_to_all(returned, 'trans', split_axis=1, concat_axis=3, tiled=True)  21.5 us
    all_to_all x1, starting transfers between devices, body(): lax.all_to_all(density, 'trans', split_axis=2, concat_axis=1, tiled=True)  19.8 us
    all_to_all x1, blocking collectives, body(): lax.all_to_all(lax.all_to_all(returned, 'trans', split_axis=1, concat_axi...  15.1 us
    all_to_all x1, starting transfers between devices, body(): lax.all_to_all(jnp.stack([summed_real, summed_imag]), 'trans', split_axis...  14.8 us
  transfers between devices with their start and end apart: 5, of which 5 were waited for; matrix products, arithmetic and copies ran while one was open for 3% of the time, Pallas kernels for 0%

commit v1 on v0

v1 whole, which is shorter than its diff:
```python
import math
import numpy as np
import jax
import jax.numpy as jnp
from jax import lax
from jax.sharding import PartitionSpec as P
from jax.experimental import pallas as pl
from jax.experimental.pallas import tpu as pltpu

BF = jnp.bfloat16
F32 = jnp.float32
N = 2048
HALF = 1024


def split_const(table):
    table = table.astype(np.float32)
    high = table.astype(BF)
    return high, (table - high.astype(np.float32)).astype(BF)


def tables():
    n2 = np.arange(128)
    k2p = np.arange(64)
    angle = 2.0 * np.pi * np.outer(n2, k2p) / 128.0
    cos, sin = np.cos(angle).reshape(128, 4, 16), np.sin(angle).reshape(128, 4, 16)
    first = np.concatenate([np.stack([cos, -sin], 2), np.stack([sin, cos], 2)], 0).reshape(256, 128)
    angle = 2.0 * np.pi * np.outer(n2, n2) / 128.0
    cos, sin = np.cos(angle), np.sin(angle)
    second = np.block([[cos, -sin], [sin, cos]])
    order = np.arange(128).reshape(64, 2).T.reshape(-1)
    back = np.block([[cos[:, order], sin[:, order]], [-sin[:, order], cos[:, order]]]) / N
    angle = 2.0 * np.pi * np.outer(k2p, n2) / 128.0
    cos, sin = np.cos(angle).reshape(4, 16, 128), np.sin(angle).reshape(4, 16, 128)
    final = np.concatenate([np.stack([cos, -sin], 1), np.stack([sin, cos], 1)], 3).reshape(128, 256) * (2.0 / N)
    swap = np.zeros((128, 128))
    swap[order, np.arange(128)] = 1.0
    angle = 2.0 * np.pi * np.outer(np.arange(16), n2) / N
    plain = np.concatenate([np.cos(angle), np.sin(angle)], 0).astype(np.float32)
    mixed = np.concatenate([np.cos(angle[:, order]), np.sin(angle[:, order])], 0).astype(np.float32)
    return first, second, back, final, swap, plain, mixed


def add(a, b):
    return b if a is None else a if b is None else a + b


def sub(a, b):
    return a if b is None else -b if a is None else a - b


def turn(value, numer, denom, sign):
    re, im = value
    eighth = (8 * numer // denom) if (8 * numer) % denom == 0 else None
    if eighth == 0:
        return value
    if eighth == 2:
        if sign == 1:
            return (None if im is None else -im, re)
        return (im, -re)
    c, s = math.cos(2 * math.pi * numer / denom), sign * math.sin(2 * math.pi * numer / denom)
    if im is None:
        return (re * c, re * s)
    if re is None:
        return (im * -s, im * c)
    return (re * c - im * s, re * s + im * c)


def short_dft(values, sign, real_out=False):
    n = len(values)
    if n == 1:
        return values
    even = short_dft(values[0::2], sign)
    odd = short_dft(values[1::2], sign)
    low, high = [], []
    for k in range(n // 2):
        t = turn(odd[k], k, n, sign)
        e = even[k]
        low.append((add(e[0], t[0]), None if real_out else add(e[1], t[1])))
        high.append((sub(e[0], t[0]), None if real_out else sub(e[1], t[1])))
    return low + high


def dot(a, b):
    return lax.dot_general(a, b, (((1,), (0,)), ((), ())), preferred_element_type=F32)


def split(x):
    high = x.astype(BF)
    return high, (x - high.astype(F32)).astype(BF)


def dot3(x, high, low):
    xh, xl = split(x)
    return dot(xh, high) + (dot(xl, high) + dot(xh, low))


def iota(shape, dim):
    return lax.broadcasted_iota(jnp.int32, shape, dim)


def wrapped(p):
    return jnp.where(p >= 1.0 * N, p - 1.0 * N, p)


def block_swap(tiles, roll):
    block = iota((8, 128), 1) // 32
    turned = {(i, d): (roll(tiles[i], 32 * d) if d else tiles[i]) for i in range(4) for d in range(4)}
    out = []
    for q in range(4):
        acc = turned[(0, (0 - q) % 4)]
        for i in range(1, 4):
            acc = jnp.where(block == i, turned[(i, (i - q) % 4)], acc)
        out.append(acc)
    return out


def columns_body(dens, pos, high, low, twid, roll, emit):
    r, c = iota((32, 32), 0), iota((32, 32), 1)
    perm = jnp.where(c == 4 * (r % 8) + r // 8, 1.0, 0.0).astype(BF)
    dens_f = dot(perm, dens)
    dens_p = dens_f.astype(BF)
    left = jnp.concatenate([dens_p[:, 256 * a : 256 * (a + 1)] for a in range(8)], axis=0)
    following = [dens_f[:, (256 * (a + 1)) % N : (256 * (a + 1)) % N + 1] for a in range(8)]
    cell = iota((256, 256), 0).astype(F32)
    tiles = []
    for v in range(8):
        p = wrapped(pos[:, 256 * v : 256 * (v + 1)])
        group = jnp.floor(p * (1.0 / 256.0))
        local = p - 256.0 * group
        table = jnp.maximum(1.0 - jnp.abs(cell - local), 0.0).astype(BF)
        edge = jnp.maximum(1.0 - jnp.abs(256.0 - local), 0.0).astype(BF).astype(F32)
        parts = dot(left, table)
        acc, nxt = parts[0:32], jnp.broadcast_to(following[0], (32, 256))
        for a in range(1, 8):
            hit = group == 1.0 * a
            acc = jnp.where(hit, parts[32 * a : 32 * (a + 1)], acc)
            nxt = jnp.where(hit, following[a], nxt)
        acc = acc + edge * nxt
        tiles += [acc[:, :128], acc[:, 128:]]
    freq = short_dft([(t, None) for t in tiles], -1)
    sign = jnp.where(iota((32, 128), 1) % 2 == 0, 1.0, -1.0)
    nyquist = jnp.sum(freq[0][0] * sign, axis=1, keepdims=True)
    for m in range(16):
        re, im = freq[m]
        if m == 0:
            zr, zi = re, jnp.zeros_like(re)
        else:
            co, si = twid[m : m + 1], twid[16 + m : 17 + m]
            im = jnp.zeros_like(re) if im is None else im
            zr, zi = re * co + im * si, im * co - re * si
        out = dot3(jnp.concatenate([zr, zi], axis=1), high, low)
        if m == 0:
            out = jnp.where(iota((32, 128), 1) == 16, nyquist, out)
        emit(m, jnp.concatenate(block_swap([out[8 * i : 8 * i + 8] for i in range(4)], roll), axis=0).astype(BF))


def rows_body(got, pos, trans, high2, low2, high3, low3, swap, twid, twid_mixed, roll, emit):
    k1p, q = trans // 4, trans % 4
    turned = got.astype(F32).T
    left = jnp.concatenate([turned, roll(turned[0:32], 511)], axis=0).astype(BF)
    cell = iota((512, 256), 0).astype(F32)
    tiles = []
    for u in range(8):
        p = wrapped(pos[:, 256 * u : 256 * (u + 1)])
        group = jnp.floor(p * 0.25)
        local = p - 4.0 * group
        table = jnp.where(cell == group, 1.0, 0.0).astype(BF)
        parts = dot(left, table)
        acc = None
        for s in range(5):
            weight = jnp.maximum(1.0 - jnp.abs(local - 1.0 * s), 0.0).astype(BF).astype(F32)
            acc = add(acc, weight * parts[32 * s : 32 * (s + 1)])
        tiles += [acc[:, :128], acc[:, 128:]]
    first = (iota((16, 128), 0) == 0) & (trans == 0)
    flat = [t[0:8] for t in tiles]
    total = flat[0]
    for t in flat[1:]:
        total = total + t
    mean = jnp.sum(total, axis=1, keepdims=True) * (1.0 / N)
    flat = dot(jnp.concatenate([t - mean for t in flat], axis=0).astype(BF), swap)
    values = []
    for t in tiles:
        re, im = t[0:16], t[16:32]
        values.append((jnp.where(first, im, re), jnp.where(first, 0.0, im)))
    freq = short_dft(values, -1)
    kappa = iota((16, 128), 0)
    lane = iota((16, 128), 1)
    k2 = 256 * q + 16 * kappa + k1p
    k2 = jnp.where(first, -HALF, k2)
    back = []
    for m in range(16):
        re, im = freq[m]
        if m:
            co, si = twid[m : m + 1], twid[16 + m : 17 + m]
            re, im = re * co + im * si, im * co - re * si
        out = dot3(jnp.concatenate([re, im], axis=1), high2, low2)
        xr, xi = out[:, :128], out[:, 128:]
        k1 = m + 16 * lane
        k1 = jnp.where(k1 >= HALF, k1 - N, k1)
        special = (k1 == -HALF) != (k2 == -HALF)
        w1, w2 = k1.astype(F32), k2.astype(F32)
        inverse = 1.0 / jnp.maximum(w1 * w1 + w2 * w2, 1.0)
        ka = (w1 * w1 - w2 * w2) * inverse
        kb = 2.0 * w1 * w2 * inverse
        odd = jnp.where(special, kb, 0.0)
        even = jnp.where(special, 0.0, kb)
        vr = jnp.concatenate([ka * xr - odd * xi, even * xr], axis=0)
        vi = jnp.concatenate([ka * xi + odd * xr, even * xi], axis=0)
        out = dot3(jnp.concatenate([vr, vi], axis=1), high3, low3)
        re, im = out[:, :128], out[:, 128:]
        if m:
            co, si = twid_mixed[m : m + 1], twid_mixed[16 + m : 17 + m]
            re, im = re * co - im * si, im * co + re * si
        back.append((re, im))
    space = short_dft(back, 1)
    low_half = iota((64, 128), 1) < 64
    zero = jnp.zeros((8, 128), F32)
    stacked = []
    for n in range(16):
        re, im = space[n]
        real0 = jnp.concatenate([flat[8 * n : 8 * n + 8], zero], axis=0)
        r0, r1, i0, i1 = re[0:16], re[16:32], im[0:16], im[16:32]
        stacked.append(
            jnp.concatenate(
                [
                    jnp.where(first, real0, r0),
                    jnp.where(first, r0, i0),
                    jnp.where(first, 0.0, r1),
                    jnp.where(first, r1, i1),
                ],
                axis=0,
            )
        )
    for m in range(8):
        a, b = stacked[2 * m], stacked[2 * m + 1]
        top = jnp.where(low_half, a, roll(b, 64))
        bottom = jnp.where(low_half, roll(a, 64), b)
        emit(m, jnp.concatenate([top, bottom], axis=0).T.astype(BF))


def final_body(load, weight, high, low, twid, roll, emit):
    row, col = iota((64, 128), 0), iota((64, 128), 1)
    slot = (iota((1, 128), 1) // 2) % 8
    mix = jnp.zeros((64, 128), F32)
    for b in range(4):
        line = jnp.zeros((1, 128), F32)
        for s in range(8):
            line = jnp.where(slot == s, weight(b, s), line)
        mix = jnp.where((row // 2) % 4 == b, line, mix)
    mix = jnp.where((row // 8 == col // 16) & (row % 2 == col % 2), mix, 0.0)
    mix_high, mix_low = split(mix)
    lane = iota((32, 128), 1)
    sign = jnp.where(lane % 2 == 0, 1.0, -1.0)
    values = []
    for block in range(8):
        got = load(block)
        summed = dot(mix_high, got) + dot(mix_low, got)
        for half in range(2):
            m = 2 * block + half
            base = 32 * half
            line = jnp.concatenate(block_swap([summed[base + 8 * i : base + 8 * i + 8] for i in range(4)], roll), axis=0)
            if m == 0:
                nyquist = line[:, 16:17]
                line = jnp.where(lane == 0, 0.5 * line, line)
            out = dot3(line, high, low)
            re, im = out[:, :128], out[:, 128:]
            if m == 0:
                values.append((re + (nyquist * (1.0 / N)) * sign, None))
            else:
                co, si = twid[m : m + 1], twid[16 + m : 17 + m]
                values.append((re * co - im * si, im * co + re * si))
    done = short_dft(values, 1, real_out=True)
    for n in range(16):
        emit(n, done[n][0])


def rolled(x, shift):
    return pltpu.roll(x, shift, 1)


def columns_kernel(plane_ref, dens_ref, pos_ref, high_ref, low_ref, twid_ref, out_ref):
    plane = plane_ref[lax.axis_index("los")]

    def emit(m, value):
        out_ref[32 * m : 32 * m + 32, :] = value

    columns_body(dens_ref[0], pos_ref[pl.ds(plane, 1), :], high_ref[...], low_ref[...], twid_ref, rolled, emit)


def rows_kernel(plane_ref, got_ref, pos_ref, high2_ref, low2_ref, high3_ref, low3_ref, swap_ref, twid_ref, mixed_ref, out_ref):
    plane = plane_ref[lax.axis_index("los")]

    def emit(m, value):
        out_ref[128 * m : 128 * m + 128, :] = value

    rows_body(
        got_ref[...],
        pos_ref[pl.ds(plane, 1), :],
        lax.axis_index("trans"),
        high2_ref[...],
        low2_ref[...],
        high3_ref[...],
        low3_ref[...],
        swap_ref[...],
        twid_ref,
        mixed_ref,
        rolled,
        emit,
    )


def final_kernel(plane_ref, bin_ref, eff_ref, got_ref, high_ref, low_ref, twid_ref, out_ref, wide_ref):
    def weight(b, s):
        plane = plane_ref[s]
        return jnp.where(b >= bin_ref[plane], eff_ref[b, plane], 0.0)

    def emit(n, value):
        for g in range(4):
            jl, comp = g // 2, g % 2
            wide_ref[n, pl.ds(16 * comp + jl, 8, stride=2), :] = value[8 * g : 8 * g + 8]

    final_body(
        lambda block: got_ref[128 * block : 128 * block + 128, :], weight, high_ref[...], low_ref[...], twid_ref, rolled, emit
    )
    for n in range(16):
        for comp in range(2):
            for b in range(4):
                base = 16 * comp + 4 * b
                out_ref[comp, b, :, 128 * n : 128 * n + 128] = wide_ref[n, base : base + 4, :]


def call(kernel, shape, dtype, scalars, arrays, scratch=()):
    smem = pl.BlockSpec(memory_space=pltpu.SMEM)
    vmem = pl.BlockSpec(memory_space=pltpu.VMEM)
    return pl.pallas_call(
        kernel,
        out_shape=jax.ShapeDtypeStruct(shape, dtype),
        in_specs=[smem] * len(scalars) + [vmem] * len(arrays),
        out_specs=vmem,
        scratch_shapes=scratch,
    )(*scalars, *arrays)


def body(density, row_pos, col_pos, plane_of_slot, plane_bin, efficiency):
    first, second, back, final, swap, plain, mixed = tables()
    swap = swap.astype(BF)
    sent = call(
        columns_kernel, (512, 128), BF, [plane_of_slot], [density, col_pos, *split_const(first), plain]
    )
    got = lax.all_to_all(sent.reshape(64, 8, 128), "trans", split_axis=0, concat_axis=0, tiled=True)
    sent = call(
        rows_kernel,
        (1024, 128),
        BF,
        [plane_of_slot],
        [got.reshape(512, 128), row_pos, *split_const(second), *split_const(back), swap, plain, mixed],
    )
    got = lax.all_to_all(sent.reshape(512, 2, 128), ("trans", "los"), split_axis=0, concat_axis=0, tiled=True)
    return call(
        final_kernel,
        (2, 4, 4, N),
        F32,
        [plane_of_slot, plane_bin, efficiency],
        [got.reshape(1024, 128), *split_const(final), plain],
        [pltpu.VMEM((16, 32, 128), F32)],
    )


def solution(mesh):
    placed = (P("los", "trans", None), P(), P(), P(), P(), P())
    return jax.shard_map(
        body,
        mesh=mesh,
        in_specs=placed,
        out_specs=P(None, None, ("trans", "los"), None),
        check_vma=False,
    )
```

time: 379 us -> 75.7 us (0.20); the launches traced: 373 us -> 75.4 us
  waiting for transfers between devices: 139 us -> 0 us
  local copies, waits for them, and re-layouts: 68.3 us -> 0 us
  matrix products: 43.9 us -> 0 us
  starting transfers between devices: 39.3 us -> 0 us
  other arithmetic: 32 us -> 0 us
  blocking collectives: 36.6 us -> 63.5 us
  between operations: 14.4 us -> 0.01 us
  Pallas kernels: 0 us -> 12 us
    reduce_scatter x2 -> x0, waiting for transfers between devices: 103 us -> none  [the longest x1 59.6 us: body(): lax.psum_scatter(term_imag, 'los', scatter_dimension=2, tiled=True)]
    dot_general x37 -> x0, matrix products: 43.9 us -> none  [the longest x4 13.3 us: body(): lax.dot_general(by_columns[local_slot], row_block, (((0,), (1,)), ((), ()...]
    all_to_all x3 -> x0, starting transfers between devices: 39.2 us -> none  [the longest x1 19.8 us: body(): lax.all_to_all(density, 'trans', split_axis=2, concat_axis=1, tiled=True)]
    all_to_all x3 -> x0, waiting for transfers between devices: 35.8 us -> none  [the longest x1 13.9 us: body(): lax.all_to_all(jnp.stack([summed_real, summed_imag]), 'trans', split_axis...]
    unnamed x20 -> x0, local copies, waits for them, and re-layouts: 32.8 us -> none
    all_to_all x2, blocking collectives: 36.6 us -> 63.5 us  [the longest x1 33.3 us: body(): lax.all_to_all(sent.reshape(64, 8, 128), 'trans', split_axis=0, concat_ax...]
    unnamed x2 -> x0, other arithmetic: 24.1 us -> none
    all_to_all x14 -> x0, local copies, waits for them, and re-layouts: 14.1 us -> none  [the longest x3 8.57 us: body(): lax.all_to_all(returned, 'trans', split_axis=1, concat_axis=3, tiled=True)]
  transfers between devices with their start and end apart: 5 -> 0, of which waited for: 5 -> 0; matrix products, arithmetic and copies ran while one was open for 3% -> 0% of each run, Pallas kernels for 0% -> 0%
where the time goes in v1:
time: 75.7 us; the launch traced here: 75.4 us
  blocking collectives  63.5 us (84%)
  Pallas kernels  12 us (16%)
    all_to_all x1, blocking collectives, body(): lax.all_to_all(sent.reshape(64, 8, 128), 'trans', split_axis=0, concat_ax...  33.3 us
    all_to_all x1, blocking collectives, body(): lax.all_to_all(sent.reshape(512, 2, 128), ('trans', 'los'), split_axis=0,...  30.2 us
    pallas_call x3, Pallas kernels, call(): pl.pallas_call(kernel, out_shape=jax.ShapeDtypeStruct(shape, dtype), in_s...  12 us

profile of v1, /device:TPU:1, one launch (start us, length us, event | category | flops | bytes accessed | tf_op | source)
XLA Modules:
  0.0 75.4 jit_solution(11457094904059125640)
XLA Ops:
  0.0 3.0 %shard_map.163 = bf16[512,128]{1,0:T(8,128)(2,1)} custom-call(s32[8]{0:T(128)} %plane_ref.5, bf16[1,32,2048]{2,1,0:T(8,128)(2,1)} %dens_ref.1, f32[8,2048]{1,0:T(8,128)} %pos_ref.2, bf16[256,128]{1,0:T(8,128)(2,1)} %constant.22.clone.high_ref, bf16[256,128]{1,0:T(8,128)(2,1)} %constant.23.clone.low_ref, f32[32,128]{1,0:T(8,128)} %constant.24.clone.twid_ref), custom_call_target="tpu_custom_call" | custom-call | tf_op jit(solution)/shard_map/pallas_call | solution.py:336
  3.0 33.3 %all_to_all.10 = bf16[64,8,128]{2,1,0:T(8,128)(2,1)} all-to-all(bf16[64,8,128]{2,1,0:T(8,128)(2,1)} %bitcast.6), channel_id=1, replica_groups=mesh['trans'=64,'los'=8] {'trans'}, dimensions={0} | all-to-all | bytes 262144 | tf_op jit(solution)/shard_map/all_to_all | solution.py:351
  36.3 4.9 %shard_map.164 = bf16[1024,128]{1,0:T(8,128)(2,1)} custom-call(s32[8]{0:T(128)} %plane_ref.5, bf16[512,128]{1,0:T(8,128)(2,1)} %bitcast.7, f32[8,2048]{1,0:T(8,128)} %pos_ref.3, bf16[256,256]{1,0:T(8,128)(2,1)} %constant.25.clone.high2_ref, bf16[256,256]{1,0:T(8,128)(2,1)} %constant.26.clone.low2_ref, bf16[256,256]{1,0:T(8,128)(2,1)} %constant.27.clone.high3_ref, ...), custom_call_target="tpu_custom_call" | custom-call | tf_op jit(solution)/shard_map/pallas_call | solution.py:336
  41.2 30.2 %all_to_all.11 = bf16[512,2,128]{2,1,0:T(2,128)(2,1)} all-to-all(bf16[512,2,128]{2,1,0:T(2,128)(2,1)} %bitcast.5), channel_id=1, replica_groups=mesh['trans'=64,'los'=8] {'trans','los'}, dimensions={0} | all-to-all | bytes 524288 | tf_op jit(solution)/shard_map/all_to_all | solution.py:359
  71.4 4.0 %shard_map.165 = f32[2,4,4,2048]{3,2,1,0:T(4,128)} custom-call(s32[8]{0:T(128)} %plane_ref.5, s32[8]{0:T(128)} %bin_ref.1, f32[4,8]{1,0:T(4,128)} %eff_ref.1, bf16[1024,128]{1,0:T(8,128)(2,1)} %bitcast.4, bf16[128,256]{1,0:T(8,128)(2,1)} %constant.31.clone.high_ref, bf16[128,256]{1,0:T(8,128)(2,1)} %constant.32.clone.low_ref, f32[32,128]{1,0:T(8,128)} %constant.24.clone.twid_ref), custom_call_target="tpu_custom_call" | custom-call | tf_op jit(solution)/shard_map/pallas_call | solution.py:336

commit v2 on v1

--- a/solution.py
+++ b/solution.py
@@ -339,6 +339,7 @@
         in_specs=[smem] * len(scalars) + [vmem] * len(arrays),
         out_specs=vmem,
         scratch_shapes=scratch,
+        compiler_params=pltpu.CompilerParams(vmem_limit_bytes=16 << 20),
     )(*scalars, *arrays)
 
 

time: 75.7 us -> 76.4 us (level)
  local copies, waits for them, and re-layouts: 0 us -> 5.49 us
  Pallas kernels: 12 us -> 9.07 us
  blocking collectives: 63.5 us -> 61.3 us
    unnamed x0 -> x34, local copies, waits for them, and re-layouts: none -> 5.49 us
    pallas_call x3, Pallas kernels: 12 us -> 9.07 us  [call(): pl.pallas_call(kernel, out_shape=jax.ShapeDtypeStruct(shape, dtype), in_s...]
    all_to_all x1, blocking collectives: 30.2 us -> 28.2 us  [body(): lax.all_to_all(sent.reshape(512, 2, 128), ('trans', 'los'), split_axis=0,...]
where the time goes in v2:
time: 76.4 us; the launch traced here: 76 us
  blocking collectives  61.3 us (80%)
  Pallas kernels  9.07 us (12%)
  local copies, waits for them, and re-layouts  5.49 us (7%)
    all_to_all x1, blocking collectives, body(): lax.all_to_all(sent.reshape(64, 8, 128), 'trans', split_axis=0, concat_ax...  33.1 us
    all_to_all x1, blocking collectives, body(): lax.all_to_all(sent.reshape(512, 2, 128), ('trans', 'los'), split_axis=0,...  28.2 us
    pallas_call x3, Pallas kernels, call(): pl.pallas_call(kernel, out_shape=jax.ShapeDtypeStruct(shape, dtype), in_s...  9.07 us
    unnamed x34, local copies, waits for them, and re-layouts  5.49 us

profile of v2, /device:TPU:1, one launch (start us, length us, event | category | flops | bytes accessed | tf_op | source)
XLA Modules:
  0.0 76.0 jit_solution(14133253182421886659)
XLA Ops:
  0.0 0.0 copy-start
  0.0 0.7 copy-done
  0.7 0.0 copy-start.1
  0.7 0.9 %copy-done.1 = bf16[1,32,2048]{2,1,0:T(8,128)(2,1)S(1)} copy-done((bf16[1,32,2048]{2,1,0:T(8,128)(2,1)S(1)}, bf16[1,32,2048]{2,1,0:T(8,128)(2,1)}, u32[]{:S(2)}) %copy-start.1) | copy-done | bytes 131096
  1.6 0.0 copy-start.6
  1.6 0.8 %copy-done.6 = f32[8,2048]{1,0:T(8,128)S(1)} copy-done((f32[8,2048]{1,0:T(8,128)S(1)}, f32[8,2048]{1,0:T(8,128)}, u32[]{:S(2)}) %copy-start.6) | copy-done | bytes 65560
  2.5 0.0 copy-start.7
  2.5 0.8 %copy-done.7 = bf16[256,128]{1,0:T(8,128)(2,1)S(1)} copy-done((bf16[256,128]{1,0:T(8,128)(2,1)S(1)}, bf16[256,128]{1,0:T(8,128)(2,1)}, u32[]{:S(2)}) %copy-start.7) | copy-done | bytes 65560
  3.3 0.0 copy-start.8
  3.3 0.8 %copy-done.8 = bf16[256,128]{1,0:T(8,128)(2,1)S(1)} copy-done((bf16[256,128]{1,0:T(8,128)(2,1)S(1)}, bf16[256,128]{1,0:T(8,128)(2,1)}, u32[]{:S(2)}) %copy-start.8) | copy-done | bytes 65560
  4.1 0.0 copy-start.14
  4.1 0.7 copy-done.14
  4.8 0.0 copy-start.4
  4.8 0.0 copy-start.5
  4.8 0.0 copy-start.11
  4.8 0.0 copy-start.12
  4.8 0.0 copy-start.13
  4.8 1.9 %shard_map.163 = bf16[512,128]{1,0:T(8,128)(2,1)S(1)} custom-call(s32[8]{0:T(128)S(1)} %copy-done.14, bf16[1,32,2048]{2,1,0:T(8,128)(2,1)S(1)} %copy-done.1, f32[8,2048]{1,0:T(8,128)S(1)} %copy-done.6, bf16[256,128]{1,0:T(8,128)(2,1)S(1)} %copy-done.8, bf16[256,128]{1,0:T(8,128)(2,1)S(1)} %copy-done.7, f32[32,128]{1,0:T(8,128)S(1)} %copy-done), custom_call_target="tpu_custom_call" | custom-call | tf_op jit(solution)/shard_map/pallas_call | solution.py:336
  6.7 0.0 copy-start.2
  6.8 0.0 copy-start.3
  6.8 33.1 %all_to_all.10 = bf16[64,8,128]{2,1,0:T(8,128)(2,1)S(1)} all-to-all(bf16[64,8,128]{2,1,0:T(8,128)(2,1)S(1)} %bitcast.6), channel_id=1, replica_groups=mesh['trans'=64,'los'=8] {'trans'}, dimensions={0} | all-to-all | bytes 262144 | tf_op jit(solution)/shard_map/all_to_all | solution.py:352
  39.9 0.0 copy-done.4
  39.9 0.0 copy-done.5
  39.9 0.0 copy-done.11
  39.9 0.0 copy-done.12
  39.9 0.0 copy-done.13
  39.9 0.0 copy-done.2
  39.9 0.0 copy-done.3
  39.9 3.6 %shard_map.164 = bf16[1024,128]{1,0:T(8,128)(2,1)S(1)} custom-call(s32[8]{0:T(128)S(1)} %copy-done.14, bf16[512,128]{1,0:T(8,128)(2,1)S(1)} %bitcast.7, f32[8,2048]{1,0:T(8,128)S(1)} %copy-done.11, bf16[256,256]{1,0:T(8,128)(2,1)S(1)} %copy-done.5, bf16[256,256]{1,0:T(8,128)(2,1)S(1)} %copy-done.4, bf16[256,256]{1,0:T(8,128)(2,1)S(1)} %copy-done.3, ...), custom_call_target="tpu_custom_call" | custom-call | tf_op jit(solution)/shard_map/pallas_call | solution.py:336
  43.5 0.0 copy-start.9
  43.5 0.0 copy-start.10
  43.5 0.0 copy-start.15
  43.5 28.2 %all_to_all.11 = bf16[512,2,128]{2,1,0:T(2,128)(2,1)S(1)} all-to-all(bf16[512,2,128]{2,1,0:T(2,128)(2,1)S(1)} %bitcast.5), channel_id=1, replica_groups=mesh['trans'=64,'los'=8] {'trans','los'}, dimensions={0} | all-to-all | bytes 524288 | tf_op jit(solution)/shard_map/all_to_all | solution.py:360
  71.8 0.0 copy-start.16
  71.8 0.0 copy-done.9
  71.8 0.0 copy-done.10
  71.8 0.0 copy-done.15
  71.8 0.6 copy-done.16
  72.4 3.6 %shard_map.165 = f32[2,4,4,2048]{3,2,1,0:T(4,128)} custom-call(s32[8]{0:T(128)S(1)} %copy-done.14, s32[8]{0:T(128)S(1)} %copy-done.16, f32[4,8]{1,0:T(4,128)S(1)} %copy-done.15, bf16[1024,128]{1,0:T(8,128)(2,1)S(1)} %bitcast.4, bf16[128,256]{1,0:T(8,128)(2,1)S(1)} %copy-done.10, bf16[128,256]{1,0:T(8,128)(2,1)S(1)} %copy-done.9, f32[32,128]{1,0:T(8,128)S(1)} %copy-done), custom_call_target="tpu_custom_call" | custom-call | tf_op jit(solution)/shard_map/pallas_call | solution.py:336
Async XLA Ops:
  0.0 0.7 copy-start
  0.7 0.9 %copy-start.1 = (bf16[1,32,2048]{2,1,0:T(8,128)(2,1)S(1)}, bf16[1,32,2048]{2,1,0:T(8,128)(2,1)}, u32[]{:S(2)}) copy-start(bf16[1,32,2048]{2,1,0:T(8,128)(2,1)} %dens_ref.1) | copy-start | bytes 393220
  1.6 0.8 %copy-start.6 = (f32[8,2048]{1,0:T(8,128)S(1)}, f32[8,2048]{1,0:T(8,128)}, u32[]{:S(2)}) copy-start(f32[8,2048]{1,0:T(8,128)} %pos_ref.2) | copy-start | bytes 196612
  2.5 0.8 %copy-start.7 = (bf16[256,128]{1,0:T(8,128)(2,1)S(1)}, bf16[256,128]{1,0:T(8,128)(2,1)}, u32[]{:S(2)}) copy-start(bf16[256,128]{1,0:T(8,128)(2,1)} %constant.23.clone.low_ref) | copy-start | bytes 196612
  3.3 0.8 %copy-start.8 = (bf16[256,128]{1,0:T(8,128)(2,1)S(1)}, bf16[256,128]{1,0:T(8,128)(2,1)}, u32[]{:S(2)}) copy-start(bf16[256,128]{1,0:T(8,128)(2,1)} %constant.22.clone.high_ref) | copy-start | bytes 196612
  4.1 0.7 copy-start.14
  4.8 35.1 %copy-start.4 = (bf16[256,256]{1,0:T(8,128)(2,1)S(1)}, bf16[256,256]{1,0:T(8,128)(2,1)}, u32[]{:S(2)}) copy-start(bf16[256,256]{1,0:T(8,128)(2,1)} %constant.26.clone.low2_ref) | copy-start | bytes 393220
  4.8 35.1 %copy-start.5 = (bf16[256,256]{1,0:T(8,128)(2,1)S(1)}, bf16[256,256]{1,0:T(8,128)(2,1)}, u32[]{:S(2)}) copy-start(bf16[256,256]{1,0:T(8,128)(2,1)} %constant.25.clone.high2_ref) | copy-start | bytes 393220
  4.8 35.1 %copy-start.11 = (f32[8,2048]{1,0:T(8,128)S(1)}, f32[8,2048]{1,0:T(8,128)}, u32[]{:S(2)}) copy-start(f32[8,2048]{1,0:T(8,128)} %pos_ref.3) | copy-start | bytes 196612
  4.8 35.1 %copy-start.12 = (bf16[128,128]{1,0:T(8,128)(2,1)S(1)}, bf16[128,128]{1,0:T(8,128)(2,1)}, u32[]{:S(2)}) copy-start(bf16[128,128]{1,0:T(8,128)(2,1)} %constant.29.clone.swap_ref) | copy-start | bytes 98308
  4.8 35.1 %copy-start.13 = (f32[32,128]{1,0:T(8,128)S(1)}, f32[32,128]{1,0:T(8,128)}, u32[]{:S(2)}) copy-start(f32[32,128]{1,0:T(8,128)} %constant.30.clone.mixed_ref) | copy-start | bytes 49156
  6.7 33.2 %copy-start.2 = (bf16[256,256]{1,0:T(8,128)(2,1)S(1)}, bf16[256,256]{1,0:T(8,128)(2,1)}, u32[]{:S(2)}) copy-start(bf16[256,256]{1,0:T(8,128)(2,1)} %constant.28.clone.low3_ref) | copy-start | bytes 393220
  6.8 33.2 %copy-start.3 = (bf16[256,256]{1,0:T(8,128)(2,1)S(1)}, bf16[256,256]{1,0:T(8,128)(2,1)}, u32[]{:S(2)}) copy-start(bf16[256,256]{1,0:T(8,128)(2,1)} %constant.27.clone.high3_ref) | copy-start | bytes 393220
  43.5 28.3 %copy-start.9 = (bf16[128,256]{1,0:T(8,128)(2,1)S(1)}, bf16[128,256]{1,0:T(8,128)(2,1)}, u32[]{:S(2)}) copy-start(bf16[128,256]{1,0:T(8,128)(2,1)} %constant.32.clone.low_ref) | copy-start | bytes 196612
  43.5 28.3 %copy-start.10 = (bf16[128,256]{1,0:T(8,128)(2,1)S(1)}, bf16[128,256]{1,0:T(8,128)(2,1)}, u32[]{:S(2)}) copy-start(bf16[128,256]{1,0:T(8,128)(2,1)} %constant.31.clone.high_ref) | copy-start | bytes 196612
  43.5 28.2 %copy-start.15 = (f32[4,8]{1,0:T(4,128)S(1)}, f32[4,8]{1,0:T(4,128)}, u32[]{:S(2)}) copy-start(f32[4,8]{1,0:T(4,128)} %eff_ref.1) | copy-start | bytes 388
  71.8 0.7 copy-start.16

commit v3 on v2

v3 whole, which is shorter than its diff:
```python
import math
import numpy as np
import jax
import jax.numpy as jnp
from jax import lax
from jax.sharding import PartitionSpec as P
from jax.experimental import pallas as pl
from jax.experimental.pallas import tpu as pltpu

BF = jnp.bfloat16
F32 = jnp.float32
N = 2048
HALF = 1024


def pair(table):
    table = table.astype(np.float32)
    high = table.astype(BF)
    return np.concatenate([high, (table - high.astype(np.float32)).astype(BF)], axis=0)


def tables():
    n2 = np.arange(128)
    k2p = np.arange(64)
    angle = 2.0 * np.pi * np.outer(n2, k2p) / 128.0
    cos, sin = np.cos(angle).reshape(128, 4, 16), np.sin(angle).reshape(128, 4, 16)
    first = np.concatenate([np.stack([cos, -sin], 2), np.stack([sin, cos], 2)], 0).reshape(256, 128)
    angle = 2.0 * np.pi * np.outer(n2, n2) / 128.0
    cos, sin = np.cos(angle), np.sin(angle)
    second = np.block([[cos, -sin], [sin, cos]])
    order = np.arange(128).reshape(64, 2).T.reshape(-1)
    back = np.block([[cos[:, order], sin[:, order]], [-sin[:, order], cos[:, order]]]) / N
    angle = 2.0 * np.pi * np.outer(k2p, n2) / 128.0
    cos, sin = np.cos(angle).reshape(4, 16, 128), np.sin(angle).reshape(4, 16, 128)
    final = np.concatenate([np.stack([cos, -sin], 1), np.stack([sin, cos], 1)], 3).reshape(128, 256) * (2.0 / N)
    swap = np.zeros((128, 128))
    swap[order, np.arange(128)] = 1.0
    angle = 2.0 * np.pi * np.outer(np.arange(16), n2) / N
    plain = np.concatenate([np.cos(angle), np.sin(angle)], 0).astype(np.float32)
    mixed = np.concatenate([np.cos(angle[:, order]), np.sin(angle[:, order])], 0).astype(np.float32)
    return first, second, back, final, swap, plain, mixed


def add(a, b):
    return b if a is None else a if b is None else a + b


def sub(a, b):
    return a if b is None else -b if a is None else a - b


def turn(value, numer, denom, sign):
    re, im = value
    eighth = (8 * numer // denom) if (8 * numer) % denom == 0 else None
    if eighth == 0:
        return value
    if eighth == 2:
        if sign == 1:
            return (None if im is None else -im, re)
        return (im, -re)
    c, s = math.cos(2 * math.pi * numer / denom), sign * math.sin(2 * math.pi * numer / denom)
    if im is None:
        return (re * c, re * s)
    if re is None:
        return (im * -s, im * c)
    return (re * c - im * s, re * s + im * c)


def short_dft(values, sign, real_out=False):
    n = len(values)
    if n == 1:
        return values
    even = short_dft(values[0::2], sign)
    odd = short_dft(values[1::2], sign)
    low, high = [], []
    for k in range(n // 2):
        t = turn(odd[k], k, n, sign)
        e = even[k]
        low.append((add(e[0], t[0]), None if real_out else add(e[1], t[1])))
        high.append((sub(e[0], t[0]), None if real_out else sub(e[1], t[1])))
    return low + high


def dot(a, b):
    return lax.dot_general(a, b, (((1,), (0,)), ((), ())), preferred_element_type=F32)


def split(x):
    high = x.astype(BF)
    return high, (x - high.astype(F32)).astype(BF)


def dot3(x, table):
    high, low = split(x)
    top = table[: x.shape[1]]
    return dot(jnp.concatenate([high, low, high], axis=1), jnp.concatenate([top, table], axis=0))


def iota(shape, dim):
    return lax.broadcasted_iota(jnp.int32, shape, dim)


def wrapped(p):
    return jnp.where(p >= 1.0 * N, p - 1.0 * N, p)


def block_swap(tiles, roll):
    block = iota((8, 128), 1) // 32
    turned = {(i, d): (roll(tiles[i], 32 * d) if d else tiles[i]) for i in range(4) for d in range(4)}
    out = []
    for q in range(4):
        acc = turned[(0, (0 - q) % 4)]
        for i in range(1, 4):
            acc = jnp.where(block == i, turned[(i, (i - q) % 4)], acc)
        out.append(acc)
    return out


def mixing(weight):
    row, col = iota((64, 128), 0), iota((64, 128), 1)
    slot = (iota((1, 128), 1) // 2) % 8
    mix = jnp.zeros((64, 128), F32)
    for b in range(4):
        line = jnp.zeros((1, 128), F32)
        for s in range(8):
            line = jnp.where(slot == s, weight(b, s), line)
        mix = jnp.where((row // 2) % 4 == b, line, mix)
    mix = jnp.where((row // 8 == col // 16) & (row % 2 == col % 2), mix, 0.0)
    return jnp.concatenate(split(mix), axis=0)


def columns_body(dens, pos, table_of, twid, roll, emit):
    r, c = iota((32, 32), 0), iota((32, 32), 1)
    perm = jnp.where(c == 4 * (r % 8) + r // 8, 1.0, 0.0).astype(BF)
    dens_f = dot(perm, dens)
    dens_p = dens_f.astype(BF)
    left = jnp.concatenate([dens_p[:, 256 * a : 256 * (a + 1)] for a in range(8)], axis=0)
    following = [dens_f[:, (256 * (a + 1)) % N : (256 * (a + 1)) % N + 1] for a in range(8)]
    cell = iota((256, 256), 0).astype(F32).astype(BF)
    zero = jnp.zeros((256, 256), BF)
    tiles = []
    for v in range(8):
        p = wrapped(pos[:, 256 * v : 256 * (v + 1)])
        group = jnp.floor(p * (1.0 / 256.0))
        local = p - 256.0 * group
        base = jnp.floor(local)
        here = (1.0 - (local - base)).astype(BF)
        there = (1.0 - (base + 1.0 - local)).astype(BF)
        table = jnp.where(cell == base.astype(BF), here, jnp.where(cell == (base + 1.0).astype(BF), there, zero))
        edge = jnp.where(base == 255.0, there.astype(F32), 0.0)
        parts = dot(left, table)
        acc, nxt = parts[0:32], jnp.broadcast_to(following[0], (32, 256))
        for a in range(1, 8):
            hit = group == 1.0 * a
            acc = jnp.where(hit, parts[32 * a : 32 * (a + 1)], acc)
            nxt = jnp.where(hit, following[a], nxt)
        acc = acc + edge * nxt
        tiles += [acc[:, :128], acc[:, 128:]]
    freq = short_dft([(t, None) for t in tiles], -1)
    lane, row = iota((32, 128), 1), iota((32, 128), 0)
    sign = jnp.where(lane % 2 == 0, 1.0, -1.0)
    nyquist = jnp.sum(freq[0][0] * sign, axis=1, keepdims=True)
    turned = []
    for m in range(16):
        re, im = freq[m]
        im = jnp.zeros_like(re) if im is None else im
        if m:
            co, si = twid[m : m + 1], twid[16 + m : 17 + m]
            re, im = re * co + im * si, im * co - re * si
        turned.append(jnp.concatenate([re, im], axis=1))
    result = dot3(jnp.concatenate(turned, axis=0), table_of())
    for m in range(16):
        out = result[32 * m : 32 * m + 32]
        if m == 0:
            base = out[0:1, 0:1].astype(BF).astype(F32)
            out = jnp.where((lane == 0) & (row > 0), out - base, jnp.where(lane == 16, nyquist, out))
        emit(m, jnp.concatenate(block_swap([out[8 * i : 8 * i + 8] for i in range(4)], roll), axis=0).astype(BF))


def rows_body(got, pos, trans, ready, twid, twid_mixed, roll, emit):
    k1p, q = trans // 4, trans % 4
    turned = got.astype(F32).T
    marked = (iota((8, 512), 0) == 0) & (iota((8, 512), 1) % 8 == 0) & (trans == 0)
    base = jnp.where(marked, turned[0:8], 0.0)
    turned = jnp.concatenate([jnp.where(marked, 0.0, turned[0:8]), turned[8:]], axis=0)
    for step in (1, 2, 4):
        base = base + roll(base, step)
    left = jnp.concatenate([turned, roll(turned[0:32], 511), base, roll(base, 511)], axis=0).astype(BF)
    cell = iota((256, 256), 0).astype(F32).astype(BF)
    one, zero = jnp.ones((256, 256), BF), jnp.zeros((256, 256), BF)
    tiles = []
    for u in range(8):
        p = wrapped(pos[:, 256 * u : 256 * (u + 1)])
        group = jnp.floor(p * 0.25)
        local = p - 4.0 * group
        table = jnp.concatenate(
            [jnp.where(cell == group.astype(BF), one, zero), jnp.where(cell == (group - 256.0).astype(BF), one, zero)], axis=0
        )
        parts = dot(left, table)
        acc = total = None
        for s in range(5):
            weight = jnp.maximum(1.0 - jnp.abs(local - 1.0 * s), 0.0).astype(BF).astype(F32)
            acc = add(acc, weight * parts[32 * s : 32 * (s + 1)])
            if s < 4:
                total = add(total, weight)
        extra = total * parts[160:168] + weight * parts[168:176]
        acc = jnp.concatenate([acc[0:8] + extra, acc[8:32]], axis=0)
        tiles += [acc[:, :128], acc[:, 128:]]
    table2, table3, swap = ready()
    first = (iota((16, 128), 0) == 0) & (trans == 0)
    flat = [t[0:8] for t in tiles]
    total = flat[0]
    for t in flat[1:]:
        total = total + t
    mean = jnp.sum(total, axis=1, keepdims=True) * (1.0 / N)
    flat = dot(jnp.concatenate([t - mean for t in flat], axis=0).astype(BF), swap)
    values = []
    for t in tiles:
        re, im = t[0:16], t[16:32]
        values.append((jnp.where(first, im, re), jnp.where(first, 0.0, im)))
    freq = short_dft(values, -1)
    turned = []
    for m in range(16):
        re, im = freq[m]
        if m:
            co, si = twid[m : m + 1], twid[16 + m : 17 + m]
            re, im = re * co + im * si, im * co - re * si
        turned.append(jnp.concatenate([re, im], axis=1))
    spectrum = dot3(jnp.concatenate(turned, axis=0), table2)
    kappa = iota((16, 128), 0)
    lane = iota((16, 128), 1)
    k2 = 256 * q + 16 * kappa + k1p
    k2 = jnp.where(first, -HALF, k2)
    w2 = k2.astype(F32)
    turned = []
    for m in range(16):
        xr, xi = spectrum[16 * m : 16 * m + 16, :128], spectrum[16 * m : 16 * m + 16, 128:]
        k1 = m + 16 * lane
        k1 = jnp.where(k1 >= HALF, k1 - N, k1)
        w1 = k1.astype(F32)
        inverse = 1.0 / jnp.maximum(w1 * w1 + w2 * w2, 1.0)
        ka = (w1 * w1 - w2 * w2) * inverse
        kb = 2.0 * w1 * w2 * inverse
        special = (k1 == -HALF) != (k2 == -HALF)
        odd = jnp.where(special, kb, 0.0)
        even = jnp.where(special, 0.0, kb)
        vr = jnp.concatenate([ka * xr - odd * xi, even * xr], axis=0)
        vi = jnp.concatenate([ka * xi + odd * xr, even * xi], axis=0)
        turned.append(jnp.concatenate([vr, vi], axis=1))
    result = dot3(jnp.concatenate(turned, axis=0), table3)
    back = []
    for m in range(16):
        re, im = result[32 * m : 32 * m + 32, :128], result[32 * m : 32 * m + 32, 128:]
        if m:
            co, si = twid_mixed[m : m + 1], twid_mixed[16 + m : 17 + m]
            re, im = re * co - im * si, im * co + re * si
        back.append((re, im))
    space = short_dft(back, 1)
    low_half = iota((64, 128), 1) < 64
    zero = jnp.zeros((8, 128), F32)
    stacked = []
    for n in range(16):
        re, im = space[n]
        real0 = jnp.concatenate([flat[8 * n : 8 * n + 8], zero], axis=0)
        r0, r1, i0, i1 = re[0:16], re[16:32], im[0:16], im[16:32]
        stacked.append(
            jnp.concatenate(
                [
                    jnp.where(first, real0, r0),
                    jnp.where(first, r0, i0),
                    jnp.where(first, 0.0, r1),
                    jnp.where(first, r1, i1),
                ],
                axis=0,
            )
        )
    for m in range(8):
        a, b = stacked[2 * m], stacked[2 * m + 1]
        top = jnp.where(low_half, a, roll(b, 64))
        bottom = jnp.where(low_half, roll(a, 64), b)
        emit(m, jnp.concatenate([top, bottom], axis=0).T.astype(BF))


def final_body(load, mix, table_of, twid, roll, emit):
    lane = iota((32, 128), 1)
    sign = jnp.where(lane % 2 == 0, 1.0, -1.0)
    lines = []
    for block in range(8):
        summed = dot(mix, load(block))
        summed = summed[0:64] + summed[64:128]
        for half in range(2):
            base = 32 * half
            line = jnp.concatenate(block_swap([summed[base + 8 * i : base + 8 * i + 8] for i in range(4)], roll), axis=0)
            if block == 0 and half == 0:
                nyquist = line[:, 16:17]
                line = jnp.where(lane == 0, 0.5 * line, line)
            lines.append(line)
    result = dot3(jnp.concatenate(lines, axis=0), table_of())
    values = []
    for m in range(16):
        re, im = result[32 * m : 32 * m + 32, :128], result[32 * m : 32 * m + 32, 128:]
        if m == 0:
            values.append((re + (nyquist * (1.0 / N)) * sign, None))
        else:
            co, si = twid[m : m + 1], twid[16 + m : 17 + m]
            values.append((re * co - im * si, im * co + re * si))
    done = short_dft(values, 1, real_out=True)
    for n in range(16):
        emit(n, done[n][0])


def rolled(x, shift):
    return pltpu.roll(x, shift, 1)


def start_copies(pairs, sems):
    copies = [pltpu.make_async_copy(src, dst, sems.at[n]) for n, (src, dst) in enumerate(pairs)]
    for copy in copies:
        copy.start()
    return copies


def columns_kernel(
    plane_hbm, bin_hbm, eff_hbm, dens_hbm, col_hbm, row_hbm, table_hbm, twid_hbm,
    out_ref, row_out, mix_out,
    plane_ref, bin_ref, eff_ref, dens_ref, col_ref, row_ref, table_ref, twid_ref, sems,
):
    pairs = [
        (plane_hbm, plane_ref), (dens_hbm, dens_ref), (col_hbm, col_ref), (twid_hbm, twid_ref),
        (table_hbm, table_ref), (row_hbm, row_ref), (bin_hbm, bin_ref), (eff_hbm, eff_ref),
    ]
    copies = start_copies(pairs, sems)
    for copy in copies[:4]:
        copy.wait()
    plane = plane_ref[lax.axis_index("los")]

    def emit(m, value):
        out_ref[32 * m : 32 * m + 32, :] = value

    def weight(b, s):
        other = plane_ref[s]
        return jnp.where(b >= bin_ref[other], eff_ref[b, other], 0.0)

    def table_of():
        for copy in copies[4:]:
            copy.wait()
        row_out[...] = row_ref[pl.ds(plane, 1), :]
        mix_out[...] = mixing(weight)
        return table_ref[...]

    columns_body(dens_ref[0], col_ref[pl.ds(plane, 1), :], table_of, twid_ref, rolled, emit)


def rows_kernel(got_ref, pos_ref, twid_ref, table2_ref, swap_ref, mixed_ref, table3_ref, out_ref):
    def emit(m, value):
        out_ref[128 * m : 128 * m + 128, :] = value

    def ready():
        return table2_ref[...], table3_ref[...], swap_ref[...]

    rows_body(got_ref[...], pos_ref[...], lax.axis_index("trans"), ready, twid_ref, mixed_ref, rolled, emit)


def final_kernel(got_ref, mix_ref, table_ref, twid_ref, out_ref, wide_ref):
    def emit(n, value):
        for g in range(4):
            jl, comp = g // 2, g % 2
            wide_ref[n, pl.ds(16 * comp + jl, 8, stride=2), :] = value[8 * g : 8 * g + 8]

    def table_of():
        return table_ref[...]

    final_body(
        lambda block: got_ref[128 * block : 128 * block + 128, :], mix_ref[...], table_of, twid_ref, rolled, emit
    )
    for n in range(16):
        for comp in range(2):
            for b in range(4):
                base = 16 * comp + 4 * b
                out_ref[comp, b, :, 128 * n : 128 * n + 128] = wide_ref[n, base : base + 4, :]


def call(kernel, shapes, near, far, scratch=()):
    vmem, hbm = (pl.BlockSpec(memory_space=m) for m in (pltpu.MemorySpace.VMEM, pltpu.MemorySpace.HBM))
    single = len(shapes) == 1
    return pl.pallas_call(
        kernel,
        out_shape=shapes[0] if single else shapes,
        in_specs=[vmem] * len(near) + [hbm] * len(far),
        out_specs=vmem if single else [vmem] * len(shapes),
        scratch_shapes=[pltpu.SMEM(a.shape, a.dtype) if a.size <= 32 else pltpu.VMEM(a.shape, a.dtype) for a in far]
        + [pltpu.SemaphoreType.DMA((len(far),))] * bool(far)
        + list(scratch),
        compiler_params=pltpu.CompilerParams(vmem_limit_bytes=16 << 20),
    )(*near, *[pltpu.with_memory_space_constraint(jnp.asarray(a), pltpu.MemorySpace.HBM) for a in far])


def body(density, row_pos, col_pos, plane_of_slot, plane_bin, efficiency):
    first, second, back, final, swap, plain, mixed = tables()
    sent, row, mix = call(
        columns_kernel,
        [jax.ShapeDtypeStruct((512, 128), BF), jax.ShapeDtypeStruct((1, N), F32), jax.ShapeDtypeStruct((128, 128), BF)],
        [],
        [plane_of_slot, plane_bin, efficiency, density, col_pos, row_pos, pair(first), plain],
    )
    got = lax.all_to_all(sent.reshape(64, 8, 128), "trans", split_axis=0, concat_axis=0, tiled=True)
    sent = call(
        rows_kernel,
        [jax.ShapeDtypeStruct((1024, 128), BF)],
        [got.reshape(512, 128), row, plain, pair(second), swap.astype(BF), mixed, pair(back)],
        [],
    )
    got = lax.all_to_all(sent.reshape(512, 2, 128), ("trans", "los"), split_axis=0, concat_axis=0, tiled=True)
    return call(
        final_kernel,
        [jax.ShapeDtypeStruct((2, 4, 4, N), F32)],
        [got.reshape(1024, 128), mix, pair(final), plain],
        [],
        [pltpu.VMEM((16, 32, 128), F32)],
    )


def solution(mesh):
    placed = (P("los", "trans", None), P(), P(), P(), P(), P())
    return jax.shard_map(
        body,
        mesh=mesh,
        in_specs=placed,
        out_specs=P(None, None, ("trans", "los"), None),
        check_vma=False,
    )
```

time: 76.4 us -> 67.5 us (0.88)
  local copies, waits for them, and re-layouts: 5.49 us -> 0.03 us
  Pallas kernels: 9.07 us -> 5.82 us
    unnamed x34 -> x12, local copies, waits for them, and re-layouts: 5.49 us -> 0.03 us
    pallas_call x3, Pallas kernels: 9.07 us -> 5.82 us  [call(): pl.pallas_call(kernel, out_shape=shapes[0] if single else shapes, in_spec...]
where the time goes in v3:
time: 67.5 us; the launch traced here: 67.3 us
  blocking collectives  61.3 us (91%)
  Pallas kernels  5.82 us (9%)
    all_to_all x1, blocking collectives, body(): lax.all_to_all(sent.reshape(64, 8, 128), 'trans', split_axis=0, concat_ax...  33.1 us
    all_to_all x1, blocking collectives, body(): lax.all_to_all(sent.reshape(512, 2, 128), ('trans', 'los'), split_axis=0,...  28.2 us
    pallas_call x3, Pallas kernels, call(): pl.pallas_call(kernel, out_shape=shapes[0] if single else shapes, in_spec...  5.82 us

profile of v3, /device:TPU:1, one launch (start us, length us, event | category | flops | bytes accessed | tf_op | source)
XLA Modules:
  0.0 67.3 jit_solution(8261218958327839421)
XLA Ops:
  0.0 0.0 copy-start
  0.0 0.0 copy-start.1
  0.0 2.4 %shard_map.127 = (bf16[512,128]{1,0:T(8,128)(2,1)S(1)}, f32[1,2048]{1,0:T(1,128)S(1)}, bf16[128,128]{1,0:T(8,128)(2,1)S(1)}) custom-call(s32[8]{0:T(128)} %plane_hbm.1, s32[8]{0:T(128)} %bin_hbm.1, f32[4,8]{1,0:T(4,128)} %eff_hbm.1, bf16[1,32,2048]{2,1,0:T(8,128)(2,1)} %dens_hbm.1, f32[8,2048]{1,0:T(8,128)} %col_hbm.1, f32[8,2048]{1,0:T(8,128)} %row_hbm.1, ...), custom_call_target="tpu_custom_call" | custom-call | tf_op jit(solution)/shard_map/pallas_call | solution.py:386
  2.4 0.0 copy-start.2
  2.4 0.0 copy-start.4
  2.4 0.0 copy-start.5
  2.5 33.1 %all_to_all.10 = bf16[64,8,128]{2,1,0:T(8,128)(2,1)S(1)} all-to-all(bf16[64,8,128]{2,1,0:T(8,128)(2,1)S(1)} %bitcast.7), channel_id=1, replica_groups=mesh['trans'=64,'los'=8] {'trans'}, dimensions={0} | all-to-all | bytes 262144 | tf_op jit(solution)/shard_map/all_to_all | solution.py:406
  35.6 0.0 copy-done
  35.6 0.0 copy-done.1
  35.6 0.0 copy-done.2
  35.6 0.0 copy-done.4
  35.6 0.0 copy-done.5
  35.6 2.0 %shard_map.128 = bf16[1024,128]{1,0:T(8,128)(2,1)S(1)} custom-call(bf16[512,128]{1,0:T(8,128)(2,1)S(1)} %bitcast.6, f32[1,2048]{1,0:T(1,128)S(1)} %get-tuple-element.9.pos_ref, f32[32,128]{1,0:T(8,128)S(1)} %copy-done.2, bf16[512,256]{1,0:T(8,128)(2,1)S(1)} %copy-done.1, bf16[128,128]{1,0:T(8,128)(2,1)S(1)} %copy-done.4, f32[32,128]{1,0:T(8,128)S(1)} %copy-done.5, ...), custom_call_target="tpu_custom_call" | custom-call | tf_op jit(solution)/shard_map/pallas_call | solution.py:386
  37.6 0.0 copy-start.3
  37.6 28.2 %all_to_all.11 = bf16[512,2,128]{2,1,0:T(2,128)(2,1)S(1)} all-to-all(bf16[512,2,128]{2,1,0:T(2,128)(2,1)S(1)} %bitcast.4), channel_id=1, replica_groups=mesh['trans'=64,'los'=8] {'trans','los'}, dimensions={0} | all-to-all | bytes 524288 | tf_op jit(solution)/shard_map/all_to_all | solution.py:413
  65.8 0.0 copy-done.3
  65.8 1.4 %shard_map.129 = f32[2,4,4,2048]{3,2,1,0:T(4,128)} custom-call(bf16[1024,128]{1,0:T(8,128)(2,1)S(1)} %bitcast.5, bf16[128,128]{1,0:T(8,128)(2,1)S(1)} %get-tuple-element.10.mix_ref, bf16[256,256]{1,0:T(8,128)(2,1)S(1)} %copy-done.3, f32[32,128]{1,0:T(8,128)S(1)} %copy-done.2), custom_call_target="tpu_custom_call" | custom-call | tf_op jit(solution)/shard_map/pallas_call | solution.py:386
Async XLA Ops:
  0.0 35.6 %copy-start = (bf16[512,256]{1,0:T(8,128)(2,1)S(1)}, bf16[512,256]{1,0:T(8,128)(2,1)}, u32[]{:S(2)}) copy-start(bf16[512,256]{1,0:T(8,128)(2,1)} %constant.19.clone.table3_ref) | copy-start | bytes 786436
  0.0 35.6 %copy-start.1 = (bf16[512,256]{1,0:T(8,128)(2,1)S(1)}, bf16[512,256]{1,0:T(8,128)(2,1)}, u32[]{:S(2)}) copy-start(bf16[512,256]{1,0:T(8,128)(2,1)} %constant.16.clone.table2_ref) | copy-start | bytes 786436
  2.4 33.2 %copy-start.2 = (f32[32,128]{1,0:T(8,128)S(1)}, f32[32,128]{1,0:T(8,128)}, u32[]{:S(2)}) copy-start(f32[32,128]{1,0:T(8,128)} %constant.15.clone.twid_hbm.twid_ref) | copy-start | bytes 49156
  2.4 33.2 %copy-start.4 = (bf16[128,128]{1,0:T(8,128)(2,1)S(1)}, bf16[128,128]{1,0:T(8,128)(2,1)}, u32[]{:S(2)}) copy-start(bf16[128,128]{1,0:T(8,128)(2,1)} %constant.17.clone.swap_ref) | copy-start | bytes 98308
  2.4 33.2 %copy-start.5 = (f32[32,128]{1,0:T(8,128)S(1)}, f32[32,128]{1,0:T(8,128)}, u32[]{:S(2)}) copy-start(f32[32,128]{1,0:T(8,128)} %constant.18.clone.mixed_ref) | copy-start | bytes 49156
  37.6 28.2 %copy-start.3 = (bf16[256,256]{1,0:T(8,128)(2,1)S(1)}, bf16[256,256]{1,0:T(8,128)(2,1)}, u32[]{:S(2)}) copy-start(bf16[256,256]{1,0:T(8,128)(2,1)} %constant.20.clone.table_ref) | copy-start | bytes 393220

commit v4 on v3

--- a/solution.py
+++ b/solution.py
@@ -11,6 +11,7 @@
 F32 = jnp.float32
 N = 2048
 HALF = 1024
+LEAD = 63
 
 
 def pair(table):
@@ -66,7 +67,7 @@
     return (re * c - im * s, re * s + im * c)
 
 
-def short_dft(values, sign, real_out=False):
+def short_dft(values, sign):
     n = len(values)
     if n == 1:
         return values
@@ -76,9 +77,45 @@
     for k in range(n // 2):
         t = turn(odd[k], k, n, sign)
         e = even[k]
-        low.append((add(e[0], t[0]), None if real_out else add(e[1], t[1])))
-        high.append((sub(e[0], t[0]), None if real_out else sub(e[1], t[1])))
+        low.append((add(e[0], t[0]), add(e[1], t[1])))
+        high.append((sub(e[0], t[0]), sub(e[1], t[1])))
     return low + high
+
+
+def real_dft(values):
+    n = len(values)
+    if n == 1:
+        return [(values[0], None)]
+    even, odd = real_dft(values[0::2]), real_dft(values[1::2])
+    if n == 2:
+        return [(even[0][0] + odd[0][0], None), (even[0][0] - odd[0][0], None)]
+    out = [None] * (n // 2 + 1)
+    for k in range(n // 4 + 1):
+        t, e = turn(odd[k], k, n, -1), even[k]
+        out[k] = (add(e[0], t[0]), add(e[1], t[1]))
+        if n // 2 - k != k:
+            out[n // 2 - k] = (sub(e[0], t[0]), sub(t[1], e[1]) if t[1] is not None else None if e[1] is None else -e[1])
+    return out
+
+
+def real_inverse(values):
+    n = 2 * len(values) - 2
+    if n == 2:
+        return [values[0][0] + values[1][0], values[0][0] - values[1][0]]
+    even, odd = [], []
+    for k in range(n // 4 + 1):
+        x, y = values[k], values[n // 2 - k]
+        if n // 2 - k == k:
+            even.append((2.0 * x[0], None))
+            odd.append((-2.0 * x[1], None))
+            continue
+        even.append((x[0] + y[0], None if k == 0 else sub(x[1], y[1])))
+        if k == 0:
+            odd.append((x[0] - y[0], None))
+        else:
+            odd.append(turn((x[0] - y[0], add(x[1], y[1])), k, n, 1))
+    even, odd = real_inverse(even), real_inverse(odd)
+    return [v for both in zip(even, odd) for v in both]
 
 
 def dot(a, b):
@@ -116,16 +153,22 @@
     return out
 
 
-def mixing(weight):
-    row, col = iota((64, 128), 0), iota((64, 128), 1)
-    slot = (iota((1, 128), 1) // 2) % 8
-    mix = jnp.zeros((64, 128), F32)
-    for b in range(4):
-        line = jnp.zeros((1, 128), F32)
-        for s in range(8):
-            line = jnp.where(slot == s, weight(b, s), line)
-        mix = jnp.where((row // 2) % 4 == b, line, mix)
-    mix = jnp.where((row // 8 == col // 16) & (row % 2 == col % 2), mix, 0.0)
+def mixing(plane_of, bin_of, eff):
+    col = iota((8, 128), 1)
+    slot = (col // 2) % 8
+    plane = jnp.zeros((8, 128), jnp.int32)
+    for s in range(8):
+        plane = jnp.where(slot == s, plane_of(s), plane)
+    first_bin = jnp.zeros((8, 128), jnp.int32)
+    weight = jnp.zeros((8, 128), F32)
+    spread = jnp.concatenate([eff[b : b + 1] for b in range(4) for _ in range(2)], axis=0)
+    for p in range(8):
+        hit = plane == p
+        first_bin = jnp.where(hit, bin_of(p), first_bin)
+        weight = jnp.where(hit, spread[:, p : p + 1], weight)
+    row = iota((8, 128), 0)
+    weight = jnp.where((row // 2 >= first_bin) & (row % 2 == col % 2), weight, 0.0)
+    mix = jnp.concatenate([jnp.where(col // 16 == t, weight, 0.0) for t in range(8)], axis=0)
     return jnp.concatenate(split(mix), axis=0)
 
 
@@ -135,6 +178,7 @@
     dens_f = dot(perm, dens)
     dens_p = dens_f.astype(BF)
     left = jnp.concatenate([dens_p[:, 256 * a : 256 * (a + 1)] for a in range(8)], axis=0)
+    lane, row = iota((32, 128), 1), iota((32, 128), 0)
     following = [dens_f[:, (256 * (a + 1)) % N : (256 * (a + 1)) % N + 1] for a in range(8)]
     cell = iota((256, 256), 0).astype(F32).astype(BF)
     zero = jnp.zeros((256, 256), BF)
@@ -156,17 +200,21 @@
             nxt = jnp.where(hit, following[a], nxt)
         acc = acc + edge * nxt
         tiles += [acc[:, :128], acc[:, 128:]]
-    freq = short_dft([(t, None) for t in tiles], -1)
-    lane, row = iota((32, 128), 1), iota((32, 128), 0)
+    freq = real_dft(tiles)
     sign = jnp.where(lane % 2 == 0, 1.0, -1.0)
     nyquist = jnp.sum(freq[0][0] * sign, axis=1, keepdims=True)
     turned = []
     for m in range(16):
-        re, im = freq[m]
-        im = jnp.zeros_like(re) if im is None else im
-        if m:
-            co, si = twid[m : m + 1], twid[16 + m : 17 + m]
+        re, im = freq[min(m, 16 - m)]
+        co, si = twid[m : m + 1], twid[16 + m : 17 + m]
+        if m == 0:
+            im = jnp.zeros_like(re)
+        elif im is None:
+            re, im = re * co, -re * si
+        elif m < 8:
             re, im = re * co + im * si, im * co - re * si
+        else:
+            re, im = re * co - im * si, -(im * co + re * si)
         turned.append(jnp.concatenate([re, im], axis=1))
     result = dot3(jnp.concatenate(turned, axis=0), table_of())
     for m in range(16):
@@ -193,8 +241,10 @@
         p = wrapped(pos[:, 256 * u : 256 * (u + 1)])
         group = jnp.floor(p * 0.25)
         local = p - 4.0 * group
+        place = group - 8.0 * LEAD
+        place = jnp.where(place < 0.0, place + 512.0, place)
         table = jnp.concatenate(
-            [jnp.where(cell == group.astype(BF), one, zero), jnp.where(cell == (group - 256.0).astype(BF), one, zero)], axis=0
+            [jnp.where(cell == place.astype(BF), one, zero), jnp.where(cell == (place - 256.0).astype(BF), one, zero)], axis=0
         )
         parts = dot(left, table)
         acc = total = None
@@ -227,25 +277,38 @@
             re, im = re * co + im * si, im * co - re * si
         turned.append(jnp.concatenate([re, im], axis=1))
     spectrum = dot3(jnp.concatenate(turned, axis=0), table2)
-    kappa = iota((16, 128), 0)
-    lane = iota((16, 128), 1)
-    k2 = 256 * q + 16 * kappa + k1p
-    k2 = jnp.where(first, -HALF, k2)
-    w2 = k2.astype(F32)
+    lane = iota((8, 128), 1)
+    top = (iota((8, 128), 0) == 0) & (trans == 0)
+    w2 = []
+    for half in range(2):
+        k2 = 256 * q + 16 * (iota((8, 128), 0) + 8 * half) + k1p
+        w2.append((jnp.where(top, -HALF, k2) if half == 0 else k2).astype(F32))
     turned = []
     for m in range(16):
-        xr, xi = spectrum[16 * m : 16 * m + 16, :128], spectrum[16 * m : 16 * m + 16, 128:]
         k1 = m + 16 * lane
-        k1 = jnp.where(k1 >= HALF, k1 - N, k1)
-        w1 = k1.astype(F32)
-        inverse = 1.0 / jnp.maximum(w1 * w1 + w2 * w2, 1.0)
-        ka = (w1 * w1 - w2 * w2) * inverse
-        kb = 2.0 * w1 * w2 * inverse
-        special = (k1 == -HALF) != (k2 == -HALF)
-        odd = jnp.where(special, kb, 0.0)
-        even = jnp.where(special, 0.0, kb)
-        vr = jnp.concatenate([ka * xr - odd * xi, even * xr], axis=0)
-        vi = jnp.concatenate([ka * xi + odd * xr, even * xi], axis=0)
+        w1 = jnp.where(k1 >= HALF, k1 - N, k1).astype(F32)
+        square, double = w1 * w1, 2.0 * w1
+        rows = [[], [], [], []]
+        for half in range(2):
+            base = 16 * m + 8 * half
+            xr, xi = spectrum[base : base + 8, :128], spectrum[base : base + 8, 128:]
+            other = w2[half] * w2[half]
+            total = square + other
+            inverse = 1.0 / (jnp.maximum(total, 1.0) if m == 0 else total)
+            ka = (square - other) * inverse
+            kb = double * w2[half] * inverse
+            pr, pi = ka * xr, ka * xi
+            if m == 0 or half == 0:
+                edge = (w1 == -1.0 * HALF) if m == 0 else None
+                if half == 0:
+                    edge = top if edge is None else edge != top
+                odd = jnp.where(edge, kb, 0.0)
+                kb = jnp.where(edge, 0.0, kb)
+                pr, pi = pr - odd * xi, pi + odd * xr
+            for part, value in zip(rows, (pr, pi, kb * xr, kb * xi)):
+                part.append(value)
+        vr = jnp.concatenate(rows[0] + rows[2], axis=0)
+        vi = jnp.concatenate(rows[1] + rows[3], axis=0)
         turned.append(jnp.concatenate([vr, vi], axis=1))
     result = dot3(jnp.concatenate(turned, axis=0), table3)
     back = []
@@ -278,7 +341,7 @@
         a, b = stacked[2 * m], stacked[2 * m + 1]
         top = jnp.where(low_half, a, roll(b, 64))
         bottom = jnp.where(low_half, roll(a, 64), b)
-        emit(m, jnp.concatenate([top, bottom], axis=0).T.astype(BF))
+        emit(m, jnp.concatenate([top, bottom], axis=0).astype(BF).T)
 
 
 def final_body(load, mix, table_of, twid, roll, emit):
@@ -304,9 +367,14 @@
         else:
             co, si = twid[m : m + 1], twid[16 + m : 17 + m]
             values.append((re * co - im * si, im * co + re * si))
-    done = short_dft(values, 1, real_out=True)
+    terms = [values[0]]
+    for m in range(1, 8):
+        x, y = values[m], values[16 - m]
+        terms.append((0.5 * (x[0] + y[0]), 0.5 * (x[1] - y[1])))
+    terms.append((values[8][0], None))
+    done = real_inverse(terms)
     for n in range(16):
-        emit(n, done[n][0])
+        emit(n, done[n])
 
 
 def rolled(x, shift):
@@ -330,22 +398,18 @@
         (table_hbm, table_ref), (row_hbm, row_ref), (bin_hbm, bin_ref), (eff_hbm, eff_ref),
     ]
     copies = start_copies(pairs, sems)
-    for copy in copies[:4]:
+    for copy in copies:
         copy.wait()
     plane = plane_ref[lax.axis_index("los")]
 
     def emit(m, value):
-        out_ref[32 * m : 32 * m + 32, :] = value
-
-    def weight(b, s):
-        other = plane_ref[s]
-        return jnp.where(b >= bin_ref[other], eff_ref[b, other], 0.0)
+        for q in range(4):
+            place = 8 * ((4 * m + q - LEAD) % 64)
+            out_ref[place : place + 8, :] = value[8 * q : 8 * q + 8]
 
     def table_of():
-        for copy in copies[4:]:
-            copy.wait()
         row_out[...] = row_ref[pl.ds(plane, 1), :]
-        mix_out[...] = mixing(weight)
+        mix_out[...] = mixing(lambda s: plane_ref[s], lambda p: bin_ref[p], eff_ref[...])
         return table_ref[...]
 
     columns_body(dens_ref[0], col_ref[pl.ds(plane, 1), :], table_of, twid_ref, rolled, emit)
@@ -388,7 +452,7 @@
         out_shape=shapes[0] if single else shapes,
         in_specs=[vmem] * len(near) + [hbm] * len(far),
         out_specs=vmem if single else [vmem] * len(shapes),
-        scratch_shapes=[pltpu.SMEM(a.shape, a.dtype) if a.size <= 32 else pltpu.VMEM(a.shape, a.dtype) for a in far]
+        scratch_shapes=[pltpu.SMEM(a.shape, a.dtype) if a.ndim == 1 else pltpu.VMEM(a.shape, a.dtype) for a in far]
         + [pltpu.SemaphoreType.DMA((len(far),))] * bool(far)
         + list(scratch),
         compiler_params=pltpu.CompilerParams(vmem_limit_bytes=16 << 20),
@@ -403,7 +467,10 @@
         [],
         [plane_of_slot, plane_bin, efficiency, density, col_pos, row_pos, pair(first), plain],
     )
-    got = lax.all_to_all(sent.reshape(64, 8, 128), "trans", split_axis=0, concat_axis=0, tiled=True)
+    order = [[(n + LEAD) % 64 for n in range(64)]]
+    got = lax.all_to_all(
+        sent.reshape(64, 8, 128), "trans", split_axis=0, concat_axis=0, tiled=True, axis_index_groups=order
+    )
     sent = call(
         rows_kernel,
         [jax.ShapeDtypeStruct((1024, 128), BF)],

time: 67.5 us -> 63.9 us (0.947)
  blocking collectives: 61.3 us -> 58 us
    all_to_all x1, blocking collectives: 33.1 us -> 26 us  [body(): lax.all_to_all(sent.reshape(64, 8, 128), 'trans', split_axis=0, concat_ax...]
    all_to_all x1, blocking collectives: 28.2 us -> 32 us  [body(): lax.all_to_all(sent.reshape(512, 2, 128), ('trans', 'los'), split_axis=0,...]
where the time goes in v4:
time: 63.9 us; the launch traced here: 63.7 us
  blocking collectives  58 us (91%)
  Pallas kernels  5.62 us (9%)
    all_to_all x1, blocking collectives, body(): lax.all_to_all(sent.reshape(512, 2, 128), ('trans', 'los'), split_axis=0,...  32 us
    all_to_all x1, blocking collectives, body(): lax.all_to_all(sent.reshape(64, 8, 128), 'trans', split_axis=0, concat_ax...  26 us
    pallas_call x3, Pallas kernels, call(): pl.pallas_call(kernel, out_shape=shapes[0] if single else shapes, in_spec...  5.62 us

profile of v4, /device:TPU:1, one launch (start us, length us, event | category | flops | bytes accessed | tf_op | source)
XLA Modules:
  0.0 63.7 jit_solution(16351749054575645346)
XLA Ops:
  0.0 0.0 copy-start
  0.0 0.0 copy-start.1
  0.0 2.3 %shard_map.127 = (bf16[512,128]{1,0:T(8,128)(2,1)S(1)}, f32[1,2048]{1,0:T(1,128)S(1)}, bf16[128,128]{1,0:T(8,128)(2,1)S(1)}) custom-call(s32[8]{0:T(128)} %plane_hbm.1, s32[8]{0:T(128)} %bin_hbm.1, f32[4,8]{1,0:T(4,128)} %eff_hbm.1, bf16[1,32,2048]{2,1,0:T(8,128)(2,1)} %dens_hbm.1, f32[8,2048]{1,0:T(8,128)} %col_hbm.1, f32[8,2048]{1,0:T(8,128)} %row_hbm.1, ...), custom_call_target="tpu_custom_call" | custom-call | tf_op jit(solution)/shard_map/pallas_call | solution.py:450
  2.3 0.0 copy-start.2
  2.4 0.0 copy-start.4
  2.4 0.0 copy-start.5
  2.4 26.0 %all_to_all.10 = bf16[64,8,128]{2,1,0:T(8,128)(2,1)S(1)} all-to-all(bf16[64,8,128]{2,1,0:T(8,128)(2,1)S(1)} %bitcast.7), channel_id=1, replica_groups={{504,0,8,16,24,32,40,48,56,64,72,80,88,96,104,112,120,128,136,144,152,1..., dimensions={0} | all-to-all | bytes 262144 | tf_op jit(solution)/shard_map/all_to_all | solution.py:471
  28.4 0.0 copy-done
  28.4 0.0 copy-done.1
  28.4 0.0 copy-done.2
  28.4 0.0 copy-done.4
  28.4 0.0 copy-done.5
  28.4 1.9 %shard_map.128 = bf16[1024,128]{1,0:T(8,128)(2,1)S(1)} custom-call(bf16[512,128]{1,0:T(8,128)(2,1)S(1)} %bitcast.6, f32[1,2048]{1,0:T(1,128)S(1)} %get-tuple-element.9.pos_ref, f32[32,128]{1,0:T(8,128)S(1)} %copy-done.2, bf16[512,256]{1,0:T(8,128)(2,1)S(1)} %copy-done.1, bf16[128,128]{1,0:T(8,128)(2,1)S(1)} %copy-done.4, f32[32,128]{1,0:T(8,128)S(1)} %copy-done.5, ...), custom_call_target="tpu_custom_call" | custom-call | tf_op jit(solution)/shard_map/pallas_call | solution.py:450
  30.3 0.0 copy-start.3
  30.3 32.0 %all_to_all.11 = bf16[512,2,128]{2,1,0:T(2,128)(2,1)S(1)} all-to-all(bf16[512,2,128]{2,1,0:T(2,128)(2,1)S(1)} %bitcast.4), channel_id=1, replica_groups=mesh['trans'=64,'los'=8] {'trans','los'}, dimensions={0} | all-to-all | bytes 524288 | tf_op jit(solution)/shard_map/all_to_all | solution.py:480
  62.3 0.0 copy-done.3
  62.3 1.4 %shard_map.129 = f32[2,4,4,2048]{3,2,1,0:T(4,128)} custom-call(bf16[1024,128]{1,0:T(8,128)(2,1)S(1)} %bitcast.5, bf16[128,128]{1,0:T(8,128)(2,1)S(1)} %get-tuple-element.10.mix_ref, bf16[256,256]{1,0:T(8,128)(2,1)S(1)} %copy-done.3, f32[32,128]{1,0:T(8,128)S(1)} %copy-done.2), custom_call_target="tpu_custom_call" | custom-call | tf_op jit(solution)/shard_map/pallas_call | solution.py:450
Async XLA Ops:
  0.0 28.4 %copy-start = (bf16[512,256]{1,0:T(8,128)(2,1)S(1)}, bf16[512,256]{1,0:T(8,128)(2,1)}, u32[]{:S(2)}) copy-start(bf16[512,256]{1,0:T(8,128)(2,1)} %constant.19.clone.table3_ref) | copy-start | bytes 786436
  0.0 28.4 %copy-start.1 = (bf16[512,256]{1,0:T(8,128)(2,1)S(1)}, bf16[512,256]{1,0:T(8,128)(2,1)}, u32[]{:S(2)}) copy-start(bf16[512,256]{1,0:T(8,128)(2,1)} %constant.16.clone.table2_ref) | copy-start | bytes 786436
  2.3 26.1 %copy-start.2 = (f32[32,128]{1,0:T(8,128)S(1)}, f32[32,128]{1,0:T(8,128)}, u32[]{:S(2)}) copy-start(f32[32,128]{1,0:T(8,128)} %constant.15.clone.twid_hbm.twid_ref) | copy-start | bytes 49156
  2.4 26.0 %copy-start.4 = (bf16[128,128]{1,0:T(8,128)(2,1)S(1)}, bf16[128,128]{1,0:T(8,128)(2,1)}, u32[]{:S(2)}) copy-start(bf16[128,128]{1,0:T(8,128)(2,1)} %constant.17.clone.swap_ref) | copy-start | bytes 98308
  2.4 26.0 %copy-start.5 = (f32[32,128]{1,0:T(8,128)S(1)}, f32[32,128]{1,0:T(8,128)}, u32[]{:S(2)}) copy-start(f32[32,128]{1,0:T(8,128)} %constant.18.clone.mixed_ref) | copy-start | bytes 49156
  30.3 32.0 %copy-start.3 = (bf16[256,256]{1,0:T(8,128)(2,1)S(1)}, bf16[256,256]{1,0:T(8,128)(2,1)}, u32[]{:S(2)}) copy-start(bf16[256,256]{1,0:T(8,128)(2,1)} %constant.20.clone.table_ref) | copy-start | bytes 393220

commit v5 on v4

--- a/solution.py
+++ b/solution.py
@@ -29,7 +29,7 @@
     angle = 2.0 * np.pi * np.outer(n2, n2) / 128.0
     cos, sin = np.cos(angle), np.sin(angle)
     second = np.block([[cos, -sin], [sin, cos]])
-    order = np.arange(128).reshape(64, 2).T.reshape(-1)
+    order = np.arange(128).reshape(32, 2, 2)[::-1].transpose(2, 0, 1).reshape(-1)
     back = np.block([[cos[:, order], sin[:, order]], [-sin[:, order], cos[:, order]]]) / N
     angle = 2.0 * np.pi * np.outer(k2p, n2) / 128.0
     cos, sin = np.cos(angle).reshape(4, 16, 128), np.sin(angle).reshape(4, 16, 128)
@@ -155,7 +155,7 @@
 
 def mixing(plane_of, bin_of, eff):
     col = iota((8, 128), 1)
-    slot = (col // 2) % 8
+    slot = 7 - (col // 2) % 8
     plane = jnp.zeros((8, 128), jnp.int32)
     for s in range(8):
         plane = jnp.where(slot == s, plane_of(s), plane)
@@ -168,7 +168,7 @@
         weight = jnp.where(hit, spread[:, p : p + 1], weight)
     row = iota((8, 128), 0)
     weight = jnp.where((row // 2 >= first_bin) & (row % 2 == col % 2), weight, 0.0)
-    mix = jnp.concatenate([jnp.where(col // 16 == t, weight, 0.0) for t in range(8)], axis=0)
+    mix = jnp.concatenate([jnp.where(col // 16 == 7 - t, weight, 0.0) for t in range(8)], axis=0)
     return jnp.concatenate(split(mix), axis=0)
 
 
@@ -338,7 +338,7 @@
             )
         )
     for m in range(8):
-        a, b = stacked[2 * m], stacked[2 * m + 1]
+        a, b = stacked[15 - 2 * m], stacked[14 - 2 * m]
         top = jnp.where(low_half, a, roll(b, 64))
         bottom = jnp.where(low_half, roll(a, 64), b)
         emit(m, jnp.concatenate([top, bottom], axis=0).astype(BF).T)
@@ -435,7 +435,7 @@
         return table_ref[...]
 
     final_body(
-        lambda block: got_ref[128 * block : 128 * block + 128, :], mix_ref[...], table_of, twid_ref, rolled, emit
+        lambda block: got_ref[128 * (7 - block) : 128 * (7 - block) + 128, :], mix_ref[...], table_of, twid_ref, rolled, emit
     )
     for n in range(16):
         for comp in range(2):
@@ -477,7 +477,10 @@
         [got.reshape(512, 128), row, plain, pair(second), swap.astype(BF), mixed, pair(back)],
         [],
     )
-    got = lax.all_to_all(sent.reshape(512, 2, 128), ("trans", "los"), split_axis=0, concat_axis=0, tiled=True)
+    order = [list(range(511, -1, -1))]
+    got = lax.all_to_all(
+        sent.reshape(512, 2, 128), ("trans", "los"), split_axis=0, concat_axis=0, tiled=True, axis_index_groups=order
+    )
     return call(
         final_kernel,
         [jax.ShapeDtypeStruct((2, 4, 4, N), F32)],

time: 63.9 us -> 63.1 us (0.987)
  blocking collectives: 58 us -> 57.1 us
    all_to_all x1, blocking collectives: 32 us -> 31.1 us  [body(): lax.all_to_all(sent.reshape(512, 2, 128), ('trans', 'los'), split_axis=0,...]
where the time goes in v5:
time: 63.1 us; the launch traced here: 62.9 us
  blocking collectives  57.1 us (90%)
  Pallas kernels  5.63 us (9%)
    all_to_all x1, blocking collectives, body(): lax.all_to_all(sent.reshape(512, 2, 128), ('trans', 'los'), split_axis=0,...  31.1 us
    all_to_all x1, blocking collectives, body(): lax.all_to_all(sent.reshape(64, 8, 128), 'trans', split_axis=0, concat_ax...  26 us
    pallas_call x3, Pallas kernels, call(): pl.pallas_call(kernel, out_shape=shapes[0] if single else shapes, in_spec...  5.63 us

profile of v5, /device:TPU:1, one launch (start us, length us, event | category | flops | bytes accessed | tf_op | source)
XLA Modules:
  0.0 62.9 jit_solution(16988172720278365028)
XLA Ops:
  0.0 0.0 copy-start
  0.0 0.0 copy-start.1
  0.0 2.3 %shard_map.127 = (bf16[512,128]{1,0:T(8,128)(2,1)S(1)}, f32[1,2048]{1,0:T(1,128)S(1)}, bf16[128,128]{1,0:T(8,128)(2,1)S(1)}) custom-call(s32[8]{0:T(128)} %plane_hbm.1, s32[8]{0:T(128)} %bin_hbm.1, f32[4,8]{1,0:T(4,128)} %eff_hbm.1, bf16[1,32,2048]{2,1,0:T(8,128)(2,1)} %dens_hbm.1, f32[8,2048]{1,0:T(8,128)} %col_hbm.1, f32[8,2048]{1,0:T(8,128)} %row_hbm.1, ...), custom_call_target="tpu_custom_call" | custom-call | tf_op jit(solution)/shard_map/pallas_call | solution.py:450
  2.3 0.0 copy-start.2
  2.4 0.0 copy-start.4
  2.4 0.0 copy-start.5
  2.4 26.0 %all_to_all.10 = bf16[64,8,128]{2,1,0:T(8,128)(2,1)S(1)} all-to-all(bf16[64,8,128]{2,1,0:T(8,128)(2,1)S(1)} %bitcast.7), channel_id=1, replica_groups={{504,0,8,16,24,32,40,48,56,64,72,80,88,96,104,112,120,128,136,144,152,1..., dimensions={0} | all-to-all | bytes 262144 | tf_op jit(solution)/shard_map/all_to_all | solution.py:471
  28.4 0.0 copy-done
  28.4 0.0 copy-done.1
  28.4 0.0 copy-done.2
  28.4 0.0 copy-done.4
  28.4 0.0 copy-done.5
  28.4 1.9 %shard_map.128 = bf16[1024,128]{1,0:T(8,128)(2,1)S(1)} custom-call(bf16[512,128]{1,0:T(8,128)(2,1)S(1)} %bitcast.6, f32[1,2048]{1,0:T(1,128)S(1)} %get-tuple-element.9.pos_ref, f32[32,128]{1,0:T(8,128)S(1)} %copy-done.2, bf16[512,256]{1,0:T(8,128)(2,1)S(1)} %copy-done.1, bf16[128,128]{1,0:T(8,128)(2,1)S(1)} %copy-done.4, f32[32,128]{1,0:T(8,128)S(1)} %copy-done.5, ...), custom_call_target="tpu_custom_call" | custom-call | tf_op jit(solution)/shard_map/pallas_call | solution.py:450
  30.3 0.0 copy-start.3
  30.3 31.1 %all_to_all.11 = bf16[512,2,128]{2,1,0:T(2,128)(2,1)S(1)} all-to-all(bf16[512,2,128]{2,1,0:T(2,128)(2,1)S(1)} %bitcast.4), channel_id=1, replica_groups={{511,510,509,508,507,506,505,504,503,502,501,500,499,498,497,496,495,49..., dimensions={0} | all-to-all | bytes 524288 | tf_op jit(solution)/shard_map/all_to_all | solution.py:481
  61.4 0.0 copy-done.3
  61.4 1.4 %shard_map.129 = f32[2,4,4,2048]{3,2,1,0:T(4,128)} custom-call(bf16[1024,128]{1,0:T(8,128)(2,1)S(1)} %bitcast.5, bf16[128,128]{1,0:T(8,128)(2,1)S(1)} %get-tuple-element.10.mix_ref, bf16[256,256]{1,0:T(8,128)(2,1)S(1)} %copy-done.3, f32[32,128]{1,0:T(8,128)S(1)} %copy-done.2), custom_call_target="tpu_custom_call" | custom-call | tf_op jit(solution)/shard_map/pallas_call | solution.py:450
Async XLA Ops:
  0.0 28.4 %copy-start = (bf16[512,256]{1,0:T(8,128)(2,1)S(1)}, bf16[512,256]{1,0:T(8,128)(2,1)}, u32[]{:S(2)}) copy-start(bf16[512,256]{1,0:T(8,128)(2,1)} %constant.19.clone.table3_ref) | copy-start | bytes 786436
  0.0 28.4 %copy-start.1 = (bf16[512,256]{1,0:T(8,128)(2,1)S(1)}, bf16[512,256]{1,0:T(8,128)(2,1)}, u32[]{:S(2)}) copy-start(bf16[512,256]{1,0:T(8,128)(2,1)} %constant.16.clone.table2_ref) | copy-start | bytes 786436
  2.3 26.1 %copy-start.2 = (f32[32,128]{1,0:T(8,128)S(1)}, f32[32,128]{1,0:T(8,128)}, u32[]{:S(2)}) copy-start(f32[32,128]{1,0:T(8,128)} %constant.15.clone.twid_hbm.twid_ref) | copy-start | bytes 49156
  2.4 26.0 %copy-start.4 = (bf16[128,128]{1,0:T(8,128)(2,1)S(1)}, bf16[128,128]{1,0:T(8,128)(2,1)}, u32[]{:S(2)}) copy-start(bf16[128,128]{1,0:T(8,128)(2,1)} %constant.17.clone.swap_ref) | copy-start | bytes 98308
  2.4 26.0 %copy-start.5 = (f32[32,128]{1,0:T(8,128)S(1)}, f32[32,128]{1,0:T(8,128)}, u32[]{:S(2)}) copy-start(f32[32,128]{1,0:T(8,128)} %constant.18.clone.mixed_ref) | copy-start | bytes 49156
  30.3 31.1 %copy-start.3 = (bf16[256,256]{1,0:T(8,128)(2,1)S(1)}, bf16[256,256]{1,0:T(8,128)(2,1)}, u32[]{:S(2)}) copy-start(bf16[256,256]{1,0:T(8,128)(2,1)} %constant.20.clone.table_ref) | copy-start | bytes 393220

commit v6 on v5

--- a/solution.py
+++ b/solution.py
@@ -29,7 +29,7 @@
     angle = 2.0 * np.pi * np.outer(n2, n2) / 128.0
     cos, sin = np.cos(angle), np.sin(angle)
     second = np.block([[cos, -sin], [sin, cos]])
-    order = np.arange(128).reshape(32, 2, 2)[::-1].transpose(2, 0, 1).reshape(-1)
+    order = np.arange(128).reshape(16, 2, 2, 2)[::-1].transpose(3, 1, 0, 2).reshape(-1)
     back = np.block([[cos[:, order], sin[:, order]], [-sin[:, order], cos[:, order]]]) / N
     angle = 2.0 * np.pi * np.outer(k2p, n2) / 128.0
     cos, sin = np.cos(angle).reshape(4, 16, 128), np.sin(angle).reshape(4, 16, 128)
@@ -153,9 +153,10 @@
     return out
 
 
-def mixing(plane_of, bin_of, eff):
+def mixing(core, plane_of, bin_of, eff):
     col = iota((8, 128), 1)
-    slot = 7 - (col // 2) % 8
+    place = (col // 2) % 8
+    slot = 2 * (3 - place // 2) + jnp.where(core == 0, place % 2, 1 - place % 2)
     plane = jnp.zeros((8, 128), jnp.int32)
     for s in range(8):
         plane = jnp.where(slot == s, plane_of(s), plane)
@@ -409,15 +410,20 @@
 
     def table_of():
         row_out[...] = row_ref[pl.ds(plane, 1), :]
-        mix_out[...] = mixing(lambda s: plane_ref[s], lambda p: bin_ref[p], eff_ref[...])
+        mix_out[...] = mixing(lax.axis_index("los") % 2, lambda s: plane_ref[s], lambda p: bin_ref[p], eff_ref[...])
         return table_ref[...]
 
     columns_body(dens_ref[0], col_ref[pl.ds(plane, 1), :], table_of, twid_ref, rolled, emit)
 
 
-def rows_kernel(got_ref, pos_ref, twid_ref, table2_ref, swap_ref, mixed_ref, table3_ref, out_ref):
+def rows_kernel(got_ref, pos_ref, twid_ref, table2_ref, swap_ref, mixed_ref, table3_ref, same_ref, other_ref):
+    north = lax.axis_index("los") % 2 == 1
+
     def emit(m, value):
-        out_ref[128 * m : 128 * m + 128, :] = value
+        zero = jnp.concatenate([value[0:32], value[64:96]], axis=0)
+        one = jnp.concatenate([value[32:64], value[96:128]], axis=0)
+        same_ref[64 * m : 64 * m + 64, :] = jnp.where(north, one, zero)
+        other_ref[64 * m : 64 * m + 64, :] = jnp.where(north, zero, one)
 
     def ready():
         return table2_ref[...], table3_ref[...], swap_ref[...]
@@ -471,16 +477,17 @@
     got = lax.all_to_all(
         sent.reshape(64, 8, 128), "trans", split_axis=0, concat_axis=0, tiled=True, axis_index_groups=order
     )
-    sent = call(
+    same, other = call(
         rows_kernel,
-        [jax.ShapeDtypeStruct((1024, 128), BF)],
+        [jax.ShapeDtypeStruct((512, 128), BF)] * 2,
         [got.reshape(512, 128), row, plain, pair(second), swap.astype(BF), mixed, pair(back)],
         [],
     )
-    order = [list(range(511, -1, -1))]
-    got = lax.all_to_all(
-        sent.reshape(512, 2, 128), ("trans", "los"), split_axis=0, concat_axis=0, tiled=True, axis_index_groups=order
-    )
+    axes = ("trans", "los")
+    other = lax.ppermute(other.reshape(256, 2, 128), axes, [(n, n ^ 1) for n in range(512)])
+    sent = jnp.concatenate([same.reshape(256, 2, 128), other], axis=1)
+    order = [[2 * n + core for n in range(255, -1, -1)] for core in range(2)]
+    got = lax.all_to_all(sent, axes, split_axis=0, concat_axis=0, tiled=True, axis_index_groups=order)
     return call(
         final_kernel,
         [jax.ShapeDtypeStruct((2, 4, 4, N), F32)],

time: 63.1 us -> 62.5 us (level)
  blocking collectives: 57.1 us -> 50.8 us
  starting transfers between devices: 0 us -> 4.04 us
  waiting for transfers between devices: 0 us -> 0.96 us
    all_to_all x1, blocking collectives: 31.1 us -> 24.8 us  [body(): lax.all_to_all(sent, axes, split_axis=0, concat_axis=0, tiled=True, axis_...]
    ppermute x0 -> x1, starting transfers between devices: none -> 4.04 us  [body(): lax.ppermute(other.reshape(256, 2, 128), axes, [(n, n ^ 1) for n in range...]
    ppermute x0 -> x1, waiting for transfers between devices: none -> 0.96 us  [body(): lax.ppermute(other.reshape(256, 2, 128), axes, [(n, n ^ 1) for n in range...]
  transfers between devices with their start and end apart: 0 -> 1, of which waited for: 0 -> 1; matrix products, arithmetic and copies ran while one was open for 0% -> 0% of each run, Pallas kernels for 0% -> 0%
where the time goes in v6:
time: 62.5 us; the launch traced here: 61.8 us
  blocking collectives  50.8 us (81%)
  Pallas kernels  5.62 us (9%)
  starting transfers between devices  4.04 us (6%)
  waiting for transfers between devices  0.96 us (2%)
    all_to_all x1, blocking collectives, body(): lax.all_to_all(sent.reshape(64, 8, 128), 'trans', split_axis=0, concat_ax...  26 us
    all_to_all x1, blocking collectives, body(): lax.all_to_all(sent, axes, split_axis=0, concat_axis=0, tiled=True, axis_...  24.8 us
    pallas_call x3, Pallas kernels, call(): pl.pallas_call(kernel, out_shape=shapes[0] if single else shapes, in_spec...  5.62 us
    ppermute x1, starting transfers between devices, body(): lax.ppermute(other.reshape(256, 2, 128), axes, [(n, n ^ 1) for n in range...  4.04 us
  transfers between devices with their start and end apart: 1, of which 1 were waited for; matrix products, arithmetic and copies ran while one was open for 0% of the time, Pallas kernels for 0%

profile of v6, /device:TPU:1, one launch (start us, length us, event | category | flops | bytes accessed | tf_op | source)
XLA Modules:
  0.0 61.8 jit_solution(2481552804551416611)
XLA Ops:
  0.0 0.0 copy-start
  0.0 0.0 copy-start.1
  0.0 2.3 %shard_map.127 = (bf16[512,128]{1,0:T(8,128)(2,1)S(1)}, f32[1,2048]{1,0:T(1,128)S(1)}, bf16[128,128]{1,0:T(8,128)(2,1)S(1)}) custom-call(s32[8]{0:T(128)} %plane_hbm.1, s32[8]{0:T(128)} %bin_hbm.1, f32[4,8]{1,0:T(4,128)} %eff_hbm.1, bf16[1,32,2048]{2,1,0:T(8,128)(2,1)} %dens_hbm.1, f32[8,2048]{1,0:T(8,128)} %col_hbm.1, f32[8,2048]{1,0:T(8,128)} %row_hbm.1, ...), custom_call_target="tpu_custom_call" | custom-call | tf_op jit(solution)/shard_map/pallas_call | solution.py:456
  2.3 0.0 copy-start.2
  2.4 0.0 copy-start.4
  2.4 0.0 copy-start.5
  2.4 26.0 %all_to_all.10 = bf16[64,8,128]{2,1,0:T(8,128)(2,1)S(1)} all-to-all(bf16[64,8,128]{2,1,0:T(8,128)(2,1)S(1)} %bitcast.7), channel_id=1, replica_groups={{504,0,8,16,24,32,40,48,56,64,72,80,88,96,104,112,120,128,136,144,152,1..., dimensions={0} | all-to-all | bytes 262144 | tf_op jit(solution)/shard_map/all_to_all | solution.py:477
  28.4 0.0 copy-done
  28.4 0.0 copy-done.1
  28.4 0.0 copy-done.2
  28.4 0.0 copy-done.4
  28.4 0.0 copy-done.5
  28.4 1.9 %shard_map.128 = (bf16[512,128]{1,0:T(8,128)(2,1)S(1)}, bf16[512,128]{1,0:T(8,128)(2,1)S(1)}) custom-call(bf16[512,128]{1,0:T(8,128)(2,1)S(1)} %bitcast.6, f32[1,2048]{1,0:T(1,128)S(1)} %get-tuple-element.11.pos_ref, f32[32,128]{1,0:T(8,128)S(1)} %copy-done.2, bf16[512,256]{1,0:T(8,128)(2,1)S(1)} %copy-done.1, bf16[128,128]{1,0:T(8,128)(2,1)S(1)} %copy-done.4, ...), custom_call_target="tpu_custom_call" | custom-call | tf_op jit(solution)/shard_map/pallas_call | solution.py:456
  30.3 4.0 %collective-permute-start = (bf16[256,2,128]{2,1,0:T(2,128)(2,1)S(1)}, bf16[256,2,128]{2,1,0:T(2,128)(2,1)S(1)}, u32[]{:S(2)}, u32[]{:S(2)}) collective-permute-start(bf16[256,2,128]{2,1,0:T(2,128)(2,1)S(1)} %bitcast.9), channel_id=1, source_target_pairs={{0,1},{1,0},{2,3},{3,2},{4,5},{5,4},{6,7},{7,6},{8,9},{9,8},{10,11... | collective-permute-start | bytes 393224 | tf_op jit(solution)/shard_map/ppermute | solution.py:487
  34.3 1.0 %collective-permute-done = bf16[256,2,128]{2,1,0:T(2,128)(2,1)S(1)} collective-permute-done((bf16[256,2,128]{2,1,0:T(2,128)(2,1)S(1)}, bf16[256,2,128]{2,1,0:T(2,128)(2,1)S(1)}, u32[]{:S(2)}, u32[]{:S(2)}) %collective-permute-start) | collective-permute-done | bytes 131104 | tf_op jit(solution)/shard_map/ppermute | solution.py:487
  35.3 0.3 pad_maximum_fusion
  35.6 0.0 copy-start.3
  35.6 24.8 %all_to_all.11 = bf16[256,4,128]{2,1,0:T(4,128)(2,1)S(1)} all-to-all(bf16[256,4,128]{2,1,0:T(4,128)(2,1)S(1)} %pad_maximum_fusion), channel_id=1, replica_groups={{510,508,506,504,502,500,498,496,494,492,490,488,486,484,482,480,478,47..., dimensions={0} | all-to-all | bytes 524288 | tf_op jit(solution)/shard_map/all_to_all | solution.py:490
  60.4 0.0 copy-done.3
  60.4 1.4 %shard_map.129 = f32[2,4,4,2048]{3,2,1,0:T(4,128)} custom-call(bf16[1024,128]{1,0:T(8,128)(2,1)S(1)} %bitcast.5, bf16[128,128]{1,0:T(8,128)(2,1)S(1)} %get-tuple-element.14.mix_ref, bf16[256,256]{1,0:T(8,128)(2,1)S(1)} %copy-done.3, f32[32,128]{1,0:T(8,128)S(1)} %copy-done.2), custom_call_target="tpu_custom_call" | custom-call | tf_op jit(solution)/shard_map/pallas_call | solution.py:456
Async XLA Ops:
  0.0 28.4 %copy-start = (bf16[512,256]{1,0:T(8,128)(2,1)S(1)}, bf16[512,256]{1,0:T(8,128)(2,1)}, u32[]{:S(2)}) copy-start(bf16[512,256]{1,0:T(8,128)(2,1)} %constant.19.clone.table3_ref) | copy-start | bytes 786436
  0.0 28.4 %copy-start.1 = (bf16[512,256]{1,0:T(8,128)(2,1)S(1)}, bf16[512,256]{1,0:T(8,128)(2,1)}, u32[]{:S(2)}) copy-start(bf16[512,256]{1,0:T(8,128)(2,1)} %constant.16.clone.table2_ref) | copy-start | bytes 786436
  2.3 26.1 %copy-start.2 = (f32[32,128]{1,0:T(8,128)S(1)}, f32[32,128]{1,0:T(8,128)}, u32[]{:S(2)}) copy-start(f32[32,128]{1,0:T(8,128)} %constant.15.clone.twid_hbm.twid_ref) | copy-start | bytes 49156
  2.4 26.0 %copy-start.4 = (bf16[128,128]{1,0:T(8,128)(2,1)S(1)}, bf16[128,128]{1,0:T(8,128)(2,1)}, u32[]{:S(2)}) copy-start(bf16[128,128]{1,0:T(8,128)(2,1)} %constant.17.clone.swap_ref) | copy-start | bytes 98308
  2.4 26.0 %copy-start.5 = (f32[32,128]{1,0:T(8,128)S(1)}, f32[32,128]{1,0:T(8,128)}, u32[]{:S(2)}) copy-start(f32[32,128]{1,0:T(8,128)} %constant.18.clone.mixed_ref) | copy-start | bytes 49156
  30.3 5.0 %collective-permute-start = (bf16[256,2,128]{2,1,0:T(2,128)(2,1)S(1)}, bf16[256,2,128]{2,1,0:T(2,128)(2,1)S(1)}, u32[]{:S(2)}, u32[]{:S(2)}) collective-permute-start(bf16[256,2,128]{2,1,0:T(2,128)(2,1)S(1)} %bitcast.9), channel_id=1, source_target_pairs={{0,1},{1,0},{2,3},{3,2},{4,5},{5,4},{6,7},{7,6},{8,9},{9,8},{10,11... | collective-permute-start | bytes 393224 | tf_op jit(solution)/shard_map/ppermute | solution.py:487
  35.6 24.8 %copy-start.3 = (bf16[256,256]{1,0:T(8,128)(2,1)S(1)}, bf16[256,256]{1,0:T(8,128)(2,1)}, u32[]{:S(2)}) copy-start(bf16[256,256]{1,0:T(8,128)(2,1)} %constant.20.clone.table_ref) | copy-start | bytes 393220

commit v7 on v6

--- a/solution.py
+++ b/solution.py
@@ -12,6 +12,7 @@
 N = 2048
 HALF = 1024
 LEAD = 63
+TOP = 7
 
 
 def pair(table):
@@ -29,7 +30,7 @@
     angle = 2.0 * np.pi * np.outer(n2, n2) / 128.0
     cos, sin = np.cos(angle), np.sin(angle)
     second = np.block([[cos, -sin], [sin, cos]])
-    order = np.arange(128).reshape(16, 2, 2, 2)[::-1].transpose(3, 1, 0, 2).reshape(-1)
+    order = np.arange(128).reshape(4, 4, 2, 2, 2)[::-1].transpose(4, 2, 0, 1, 3).reshape(-1)
     back = np.block([[cos[:, order], sin[:, order]], [-sin[:, order], cos[:, order]]]) / N
     angle = 2.0 * np.pi * np.outer(k2p, n2) / 128.0
     cos, sin = np.cos(angle).reshape(4, 16, 128), np.sin(angle).reshape(4, 16, 128)
@@ -156,7 +157,7 @@
 def mixing(core, plane_of, bin_of, eff):
     col = iota((8, 128), 1)
     place = (col // 2) % 8
-    slot = 2 * (3 - place // 2) + jnp.where(core == 0, place % 2, 1 - place % 2)
+    slot = 2 * (place // 2) + jnp.where(core == 0, place % 2, 1 - place % 2)
     plane = jnp.zeros((8, 128), jnp.int32)
     for s in range(8):
         plane = jnp.where(slot == s, plane_of(s), plane)
@@ -339,7 +340,8 @@
             )
         )
     for m in range(8):
-        a, b = stacked[15 - 2 * m], stacked[14 - 2 * m]
+        block = (TOP - m) % 8
+        a, b = stacked[2 * block + 1], stacked[2 * block]
         top = jnp.where(low_half, a, roll(b, 64))
         bottom = jnp.where(low_half, roll(a, 64), b)
         emit(m, jnp.concatenate([top, bottom], axis=0).astype(BF).T)
@@ -441,7 +443,7 @@
         return table_ref[...]
 
     final_body(
-        lambda block: got_ref[128 * (7 - block) : 128 * (7 - block) + 128, :], mix_ref[...], table_of, twid_ref, rolled, emit
+        lambda block: got_ref[pl.ds(128 * ((TOP - block) % 8), 128), :], mix_ref[...], table_of, twid_ref, rolled, emit
     )
     for n in range(16):
         for comp in range(2):
@@ -486,7 +488,8 @@
     axes = ("trans", "los")
     other = lax.ppermute(other.reshape(256, 2, 128), axes, [(n, n ^ 1) for n in range(512)])
     sent = jnp.concatenate([same.reshape(256, 2, 128), other], axis=1)
-    order = [[2 * n + core for n in range(255, -1, -1)] for core in range(2)]
+    chips = [32 * ((TOP - m) % 8) + 28 - 4 * t + n for m in range(8) for t in range(8) for n in range(4)]
+    order = [[2 * n + core for n in chips] for core in range(2)]
     got = lax.all_to_all(sent, axes, split_axis=0, concat_axis=0, tiled=True, axis_index_groups=order)
     return call(
         final_kernel,

time: 62.5 us -> 61.8 us (0.989)
  blocking collectives: 50.8 us -> 50 us
    all_to_all x1, blocking collectives: 24.8 us -> 24 us  [body(): lax.all_to_all(sent, axes, split_axis=0, concat_axis=0, tiled=True, axis_...]
where the time goes in v7:
time: 61.8 us; the launch traced here: 61 us
  blocking collectives  50 us (81%)
  Pallas kernels  5.62 us (9%)
  starting transfers between devices  4.04 us (7%)
  waiting for transfers between devices  0.96 us (2%)
    all_to_all x1, blocking collectives, body(): lax.all_to_all(sent.reshape(64, 8, 128), 'trans', split_axis=0, concat_ax...  26 us
    all_to_all x1, blocking collectives, body(): lax.all_to_all(sent, axes, split_axis=0, concat_axis=0, tiled=True, axis_...  24 us
    pallas_call x3, Pallas kernels, call(): pl.pallas_call(kernel, out_shape=shapes[0] if single else shapes, in_spec...  5.62 us
    ppermute x1, starting transfers between devices, body(): lax.ppermute(other.reshape(256, 2, 128), axes, [(n, n ^ 1) for n in range...  4.04 us
  transfers between devices with their start and end apart: 1, of which 1 were waited for; matrix products, arithmetic and copies ran while one was open for 0% of the time, Pallas kernels for 0%

profile of v7, /device:TPU:1, one launch (start us, length us, event | category | flops | bytes accessed | tf_op | source)
XLA Modules:
  0.0 61.0 jit_solution(9285808890618689394)
XLA Ops:
  0.0 0.0 copy-start
  0.0 0.0 copy-start.1
  0.0 2.3 %shard_map.127 = (bf16[512,128]{1,0:T(8,128)(2,1)S(1)}, f32[1,2048]{1,0:T(1,128)S(1)}, bf16[128,128]{1,0:T(8,128)(2,1)S(1)}) custom-call(s32[8]{0:T(128)} %plane_hbm.1, s32[8]{0:T(128)} %bin_hbm.1, f32[4,8]{1,0:T(4,128)} %eff_hbm.1, bf16[1,32,2048]{2,1,0:T(8,128)(2,1)} %dens_hbm.1, f32[8,2048]{1,0:T(8,128)} %col_hbm.1, f32[8,2048]{1,0:T(8,128)} %row_hbm.1, ...), custom_call_target="tpu_custom_call" | custom-call | tf_op jit(solution)/shard_map/pallas_call | solution.py:458
  2.3 0.0 copy-start.2
  2.4 0.0 copy-start.4
  2.4 0.0 copy-start.5
  2.4 26.0 %all_to_all.10 = bf16[64,8,128]{2,1,0:T(8,128)(2,1)S(1)} all-to-all(bf16[64,8,128]{2,1,0:T(8,128)(2,1)S(1)} %bitcast.7), channel_id=1, replica_groups={{504,0,8,16,24,32,40,48,56,64,72,80,88,96,104,112,120,128,136,144,152,1..., dimensions={0} | all-to-all | bytes 262144 | tf_op jit(solution)/shard_map/all_to_all | solution.py:479
  28.4 0.0 copy-done
  28.4 0.0 copy-done.1
  28.4 0.0 copy-done.2
  28.4 0.0 copy-done.4
  28.4 0.0 copy-done.5
  28.4 1.9 %shard_map.128 = (bf16[512,128]{1,0:T(8,128)(2,1)S(1)}, bf16[512,128]{1,0:T(8,128)(2,1)S(1)}) custom-call(bf16[512,128]{1,0:T(8,128)(2,1)S(1)} %bitcast.6, f32[1,2048]{1,0:T(1,128)S(1)} %get-tuple-element.11.pos_ref, f32[32,128]{1,0:T(8,128)S(1)} %copy-done.2, bf16[512,256]{1,0:T(8,128)(2,1)S(1)} %copy-done.1, bf16[128,128]{1,0:T(8,128)(2,1)S(1)} %copy-done.4, ...), custom_call_target="tpu_custom_call" | custom-call | tf_op jit(solution)/shard_map/pallas_call | solution.py:458
  30.3 4.0 %collective-permute-start = (bf16[256,2,128]{2,1,0:T(2,128)(2,1)S(1)}, bf16[256,2,128]{2,1,0:T(2,128)(2,1)S(1)}, u32[]{:S(2)}, u32[]{:S(2)}) collective-permute-start(bf16[256,2,128]{2,1,0:T(2,128)(2,1)S(1)} %bitcast.9), channel_id=1, source_target_pairs={{0,1},{1,0},{2,3},{3,2},{4,5},{5,4},{6,7},{7,6},{8,9},{9,8},{10,11... | collective-permute-start | bytes 393224 | tf_op jit(solution)/shard_map/ppermute | solution.py:489
  34.3 1.0 %collective-permute-done = bf16[256,2,128]{2,1,0:T(2,128)(2,1)S(1)} collective-permute-done((bf16[256,2,128]{2,1,0:T(2,128)(2,1)S(1)}, bf16[256,2,128]{2,1,0:T(2,128)(2,1)S(1)}, u32[]{:S(2)}, u32[]{:S(2)}) %collective-permute-start) | collective-permute-done | bytes 131104 | tf_op jit(solution)/shard_map/ppermute | solution.py:489
  35.3 0.3 pad_maximum_fusion
  35.6 0.0 copy-start.3
  35.6 24.0 %all_to_all.11 = bf16[256,4,128]{2,1,0:T(4,128)(2,1)S(1)} all-to-all(bf16[256,4,128]{2,1,0:T(4,128)(2,1)S(1)} %pad_maximum_fusion), channel_id=1, replica_groups={{504,506,508,510,496,498,500,502,488,490,492,494,480,482,484,486,472,47..., dimensions={0} | all-to-all | bytes 524288 | tf_op jit(solution)/shard_map/all_to_all | solution.py:493
  59.6 0.0 copy-done.3
  59.6 1.4 %shard_map.129 = f32[2,4,4,2048]{3,2,1,0:T(4,128)} custom-call(bf16[1024,128]{1,0:T(8,128)(2,1)S(1)} %bitcast.5, bf16[128,128]{1,0:T(8,128)(2,1)S(1)} %get-tuple-element.14.mix_ref, bf16[256,256]{1,0:T(8,128)(2,1)S(1)} %copy-done.3, f32[32,128]{1,0:T(8,128)S(1)} %copy-done.2), custom_call_target="tpu_custom_call" | custom-call | tf_op jit(solution)/shard_map/pallas_call | solution.py:458
Async XLA Ops:
  0.0 28.4 %copy-start = (bf16[512,256]{1,0:T(8,128)(2,1)S(1)}, bf16[512,256]{1,0:T(8,128)(2,1)}, u32[]{:S(2)}) copy-start(bf16[512,256]{1,0:T(8,128)(2,1)} %constant.19.clone.table3_ref) | copy-start | bytes 786436
  0.0 28.4 %copy-start.1 = (bf16[512,256]{1,0:T(8,128)(2,1)S(1)}, bf16[512,256]{1,0:T(8,128)(2,1)}, u32[]{:S(2)}) copy-start(bf16[512,256]{1,0:T(8,128)(2,1)} %constant.16.clone.table2_ref) | copy-start | bytes 786436
  2.3 26.0 %copy-start.2 = (f32[32,128]{1,0:T(8,128)S(1)}, f32[32,128]{1,0:T(8,128)}, u32[]{:S(2)}) copy-start(f32[32,128]{1,0:T(8,128)} %constant.15.clone.twid_hbm.twid_ref) | copy-start | bytes 49156
  2.4 26.0 %copy-start.4 = (bf16[128,128]{1,0:T(8,128)(2,1)S(1)}, bf16[128,128]{1,0:T(8,128)(2,1)}, u32[]{:S(2)}) copy-start(bf16[128,128]{1,0:T(8,128)(2,1)} %constant.17.clone.swap_ref) | copy-start | bytes 98308
  2.4 26.0 %copy-start.5 = (f32[32,128]{1,0:T(8,128)S(1)}, f32[32,128]{1,0:T(8,128)}, u32[]{:S(2)}) copy-start(f32[32,128]{1,0:T(8,128)} %constant.18.clone.mixed_ref) | copy-start | bytes 49156
  30.3 5.0 %collective-permute-start = (bf16[256,2,128]{2,1,0:T(2,128)(2,1)S(1)}, bf16[256,2,128]{2,1,0:T(2,128)(2,1)S(1)}, u32[]{:S(2)}, u32[]{:S(2)}) collective-permute-start(bf16[256,2,128]{2,1,0:T(2,128)(2,1)S(1)} %bitcast.9), channel_id=1, source_target_pairs={{0,1},{1,0},{2,3},{3,2},{4,5},{5,4},{6,7},{7,6},{8,9},{9,8},{10,11... | collective-permute-start | bytes 393224 | tf_op jit(solution)/shard_map/ppermute | solution.py:489
  35.6 24.0 %copy-start.3 = (bf16[256,256]{1,0:T(8,128)(2,1)S(1)}, bf16[256,256]{1,0:T(8,128)(2,1)}, u32[]{:S(2)}) copy-start(bf16[256,256]{1,0:T(8,128)(2,1)} %constant.20.clone.table_ref) | copy-start | bytes 393220

commit v8 on v7

--- a/solution.py
+++ b/solution.py
@@ -496,7 +496,7 @@
         [jax.ShapeDtypeStruct((2, 4, 4, N), F32)],
         [got.reshape(1024, 128), mix, pair(final), plain],
         [],
-        [pltpu.VMEM((16, 32, 128), F32)],
+        [pltpu.VMEM((16, 40, 128), F32)],
     )
 
 

time: 61.8 us -> 61.8 us (level)
  no operation moved by 1% of the time
where the time goes in v8:
time: 61.8 us; the launch traced here: 61 us
  blocking collectives  50 us (81%)
  Pallas kernels  5.62 us (9%)
  starting transfers between devices  4.04 us (7%)
  waiting for transfers between devices  0.96 us (2%)
    all_to_all x1, blocking collectives, body(): lax.all_to_all(sent.reshape(64, 8, 128), 'trans', split_axis=0, concat_ax...  26 us
    all_to_all x1, blocking collectives, body(): lax.all_to_all(sent, axes, split_axis=0, concat_axis=0, tiled=True, axis_...  24 us
    pallas_call x3, Pallas kernels, call(): pl.pallas_call(kernel, out_shape=shapes[0] if single else shapes, in_spec...  5.62 us
    ppermute x1, starting transfers between devices, body(): lax.ppermute(other.reshape(256, 2, 128), axes, [(n, n ^ 1) for n in range...  4.04 us
  transfers between devices with their start and end apart: 1, of which 1 were waited for; matrix products, arithmetic and copies ran while one was open for 0% of the time, Pallas kernels for 0%

profile of v8, /device:TPU:1, one launch (start us, length us, event | category | flops | bytes accessed | tf_op | source)
XLA Modules:
  0.0 61.0 jit_solution(8539327767365395661)
XLA Ops:
  0.0 0.0 copy-start
  0.0 0.0 copy-start.1
  0.0 2.3 %shard_map.127 = (bf16[512,128]{1,0:T(8,128)(2,1)S(1)}, f32[1,2048]{1,0:T(1,128)S(1)}, bf16[128,128]{1,0:T(8,128)(2,1)S(1)}) custom-call(s32[8]{0:T(128)} %plane_hbm.1, s32[8]{0:T(128)} %bin_hbm.1, f32[4,8]{1,0:T(4,128)} %eff_hbm.1, bf16[1,32,2048]{2,1,0:T(8,128)(2,1)} %dens_hbm.1, f32[8,2048]{1,0:T(8,128)} %col_hbm.1, f32[8,2048]{1,0:T(8,128)} %row_hbm.1, ...), custom_call_target="tpu_custom_call" | custom-call | tf_op jit(solution)/shard_map/pallas_call | solution.py:458
  2.3 0.0 copy-start.2
  2.4 0.0 copy-start.4
  2.4 0.0 copy-start.5
  2.4 26.0 %all_to_all.10 = bf16[64,8,128]{2,1,0:T(8,128)(2,1)S(1)} all-to-all(bf16[64,8,128]{2,1,0:T(8,128)(2,1)S(1)} %bitcast.7), channel_id=1, replica_groups={{504,0,8,16,24,32,40,48,56,64,72,80,88,96,104,112,120,128,136,144,152,1..., dimensions={0} | all-to-all | bytes 262144 | tf_op jit(solution)/shard_map/all_to_all | solution.py:479
  28.4 0.0 copy-done
  28.4 0.0 copy-done.1
  28.4 0.0 copy-done.2
  28.4 0.0 copy-done.4
  28.4 0.0 copy-done.5
  28.4 1.9 %shard_map.128 = (bf16[512,128]{1,0:T(8,128)(2,1)S(1)}, bf16[512,128]{1,0:T(8,128)(2,1)S(1)}) custom-call(bf16[512,128]{1,0:T(8,128)(2,1)S(1)} %bitcast.6, f32[1,2048]{1,0:T(1,128)S(1)} %get-tuple-element.11.pos_ref, f32[32,128]{1,0:T(8,128)S(1)} %copy-done.2, bf16[512,256]{1,0:T(8,128)(2,1)S(1)} %copy-done.1, bf16[128,128]{1,0:T(8,128)(2,1)S(1)} %copy-done.4, ...), custom_call_target="tpu_custom_call" | custom-call | tf_op jit(solution)/shard_map/pallas_call | solution.py:458
  30.3 4.0 %collective-permute-start = (bf16[256,2,128]{2,1,0:T(2,128)(2,1)S(1)}, bf16[256,2,128]{2,1,0:T(2,128)(2,1)S(1)}, u32[]{:S(2)}, u32[]{:S(2)}) collective-permute-start(bf16[256,2,128]{2,1,0:T(2,128)(2,1)S(1)} %bitcast.9), channel_id=1, source_target_pairs={{0,1},{1,0},{2,3},{3,2},{4,5},{5,4},{6,7},{7,6},{8,9},{9,8},{10,11... | collective-permute-start | bytes 393224 | tf_op jit(solution)/shard_map/ppermute | solution.py:489
  34.3 1.0 %collective-permute-done = bf16[256,2,128]{2,1,0:T(2,128)(2,1)S(1)} collective-permute-done((bf16[256,2,128]{2,1,0:T(2,128)(2,1)S(1)}, bf16[256,2,128]{2,1,0:T(2,128)(2,1)S(1)}, u32[]{:S(2)}, u32[]{:S(2)}) %collective-permute-start) | collective-permute-done | bytes 131104 | tf_op jit(solution)/shard_map/ppermute | solution.py:489
  35.3 0.3 pad_maximum_fusion
  35.6 0.0 copy-start.3
  35.6 24.0 %all_to_all.11 = bf16[256,4,128]{2,1,0:T(4,128)(2,1)S(1)} all-to-all(bf16[256,4,128]{2,1,0:T(4,128)(2,1)S(1)} %pad_maximum_fusion), channel_id=1, replica_groups={{504,506,508,510,496,498,500,502,488,490,492,494,480,482,484,486,472,47..., dimensions={0} | all-to-all | bytes 524288 | tf_op jit(solution)/shard_map/all_to_all | solution.py:493
  59.6 0.0 copy-done.3
  59.6 1.4 %shard_map.129 = f32[2,4,4,2048]{3,2,1,0:T(4,128)} custom-call(bf16[1024,128]{1,0:T(8,128)(2,1)S(1)} %bitcast.5, bf16[128,128]{1,0:T(8,128)(2,1)S(1)} %get-tuple-element.14.mix_ref, bf16[256,256]{1,0:T(8,128)(2,1)S(1)} %copy-done.3, f32[32,128]{1,0:T(8,128)S(1)} %copy-done.2), custom_call_target="tpu_custom_call" | custom-call | tf_op jit(solution)/shard_map/pallas_call | solution.py:458
Async XLA Ops:
  0.0 28.4 %copy-start = (bf16[512,256]{1,0:T(8,128)(2,1)S(1)}, bf16[512,256]{1,0:T(8,128)(2,1)}, u32[]{:S(2)}) copy-start(bf16[512,256]{1,0:T(8,128)(2,1)} %constant.19.clone.table3_ref) | copy-start | bytes 786436
  0.0 28.4 %copy-start.1 = (bf16[512,256]{1,0:T(8,128)(2,1)S(1)}, bf16[512,256]{1,0:T(8,128)(2,1)}, u32[]{:S(2)}) copy-start(bf16[512,256]{1,0:T(8,128)(2,1)} %constant.16.clone.table2_ref) | copy-start | bytes 786436
  2.3 26.0 %copy-start.2 = (f32[32,128]{1,0:T(8,128)S(1)}, f32[32,128]{1,0:T(8,128)}, u32[]{:S(2)}) copy-start(f32[32,128]{1,0:T(8,128)} %constant.15.clone.twid_hbm.twid_ref) | copy-start | bytes 49156
  2.4 26.0 %copy-start.4 = (bf16[128,128]{1,0:T(8,128)(2,1)S(1)}, bf16[128,128]{1,0:T(8,128)(2,1)}, u32[]{:S(2)}) copy-start(bf16[128,128]{1,0:T(8,128)(2,1)} %constant.17.clone.swap_ref) | copy-start | bytes 98308
  2.4 26.0 %copy-start.5 = (f32[32,128]{1,0:T(8,128)S(1)}, f32[32,128]{1,0:T(8,128)}, u32[]{:S(2)}) copy-start(f32[32,128]{1,0:T(8,128)} %constant.18.clone.mixed_ref) | copy-start | bytes 49156
  30.3 5.0 %collective-permute-start = (bf16[256,2,128]{2,1,0:T(2,128)(2,1)S(1)}, bf16[256,2,128]{2,1,0:T(2,128)(2,1)S(1)}, u32[]{:S(2)}, u32[]{:S(2)}) collective-permute-start(bf16[256,2,128]{2,1,0:T(2,128)(2,1)S(1)} %bitcast.9), channel_id=1, source_target_pairs={{0,1},{1,0},{2,3},{3,2},{4,5},{5,4},{6,7},{7,6},{8,9},{9,8},{10,11... | collective-permute-start | bytes 393224 | tf_op jit(solution)/shard_map/ppermute | solution.py:489
  35.6 24.0 %copy-start.3 = (bf16[256,256]{1,0:T(8,128)(2,1)S(1)}, bf16[256,256]{1,0:T(8,128)(2,1)}, u32[]{:S(2)}) copy-start(bf16[256,256]{1,0:T(8,128)(2,1)} %constant.20.clone.table_ref) | copy-start | bytes 393220

commit v9 on v8

--- a/solution.py
+++ b/solution.py
@@ -401,7 +401,7 @@
         (table_hbm, table_ref), (row_hbm, row_ref), (bin_hbm, bin_ref), (eff_hbm, eff_ref),
     ]
     copies = start_copies(pairs, sems)
-    for copy in copies:
+    for copy in copies[:4]:
         copy.wait()
     plane = plane_ref[lax.axis_index("los")]
 
@@ -411,6 +411,8 @@
             out_ref[place : place + 8, :] = value[8 * q : 8 * q + 8]
 
     def table_of():
+        for copy in copies[4:]:
+            copy.wait()
         row_out[...] = row_ref[pl.ds(plane, 1), :]
         mix_out[...] = mixing(lax.axis_index("los") % 2, lambda s: plane_ref[s], lambda p: bin_ref[p], eff_ref[...])
         return table_ref[...]

time: 61.8 us -> 61.9 us (level)
  no operation moved by 1% of the time
where the time goes in v9:
time: 61.9 us; the launch traced here: 61.1 us
  blocking collectives  50 us (81%)
  Pallas kernels  5.67 us (9%)
  starting transfers between devices  4.04 us (7%)
  waiting for transfers between devices  0.96 us (2%)
    all_to_all x1, blocking collectives, body(): lax.all_to_all(sent.reshape(64, 8, 128), 'trans', split_axis=0, concat_ax...  26 us
    all_to_all x1, blocking collectives, body(): lax.all_to_all(sent, axes, split_axis=0, concat_axis=0, tiled=True, axis_...  24 us
    pallas_call x3, Pallas kernels, call(): pl.pallas_call(kernel, out_shape=shapes[0] if single else shapes, in_spec...  5.67 us
    ppermute x1, starting transfers between devices, body(): lax.ppermute(other.reshape(256, 2, 128), axes, [(n, n ^ 1) for n in range...  4.04 us
  transfers between devices with their start and end apart: 1, of which 1 were waited for; matrix products, arithmetic and copies ran while one was open for 0% of the time, Pallas kernels for 0%

profile of v9, /device:TPU:1, one launch (start us, length us, event | category | flops | bytes accessed | tf_op | source)
XLA Modules:
  0.0 61.1 jit_solution(10201011478698664524)
XLA Ops:
  0.0 0.0 copy-start
  0.0 0.0 copy-start.1
  0.0 2.4 %shard_map.127 = (bf16[512,128]{1,0:T(8,128)(2,1)S(1)}, f32[1,2048]{1,0:T(1,128)S(1)}, bf16[128,128]{1,0:T(8,128)(2,1)S(1)}) custom-call(s32[8]{0:T(128)} %plane_hbm.1, s32[8]{0:T(128)} %bin_hbm.1, f32[4,8]{1,0:T(4,128)} %eff_hbm.1, bf16[1,32,2048]{2,1,0:T(8,128)(2,1)} %dens_hbm.1, f32[8,2048]{1,0:T(8,128)} %col_hbm.1, f32[8,2048]{1,0:T(8,128)} %row_hbm.1, ...), custom_call_target="tpu_custom_call" | custom-call | tf_op jit(solution)/shard_map/pallas_call | solution.py:460
  2.4 0.0 copy-start.2
  2.4 0.0 copy-start.4
  2.4 0.0 copy-start.5
  2.4 26.0 %all_to_all.10 = bf16[64,8,128]{2,1,0:T(8,128)(2,1)S(1)} all-to-all(bf16[64,8,128]{2,1,0:T(8,128)(2,1)S(1)} %bitcast.7), channel_id=1, replica_groups={{504,0,8,16,24,32,40,48,56,64,72,80,88,96,104,112,120,128,136,144,152,1..., dimensions={0} | all-to-all | bytes 262144 | tf_op jit(solution)/shard_map/all_to_all | solution.py:481
  28.4 0.0 copy-done
  28.4 0.0 copy-done.1
  28.4 0.0 copy-done.2
  28.4 0.0 copy-done.4
  28.4 0.0 copy-done.5
  28.5 1.9 %shard_map.128 = (bf16[512,128]{1,0:T(8,128)(2,1)S(1)}, bf16[512,128]{1,0:T(8,128)(2,1)S(1)}) custom-call(bf16[512,128]{1,0:T(8,128)(2,1)S(1)} %bitcast.6, f32[1,2048]{1,0:T(1,128)S(1)} %get-tuple-element.11.pos_ref, f32[32,128]{1,0:T(8,128)S(1)} %copy-done.2, bf16[512,256]{1,0:T(8,128)(2,1)S(1)} %copy-done.1, bf16[128,128]{1,0:T(8,128)(2,1)S(1)} %copy-done.4, ...), custom_call_target="tpu_custom_call" | custom-call | tf_op jit(solution)/shard_map/pallas_call | solution.py:460
  30.3 4.0 %collective-permute-start = (bf16[256,2,128]{2,1,0:T(2,128)(2,1)S(1)}, bf16[256,2,128]{2,1,0:T(2,128)(2,1)S(1)}, u32[]{:S(2)}, u32[]{:S(2)}) collective-permute-start(bf16[256,2,128]{2,1,0:T(2,128)(2,1)S(1)} %bitcast.9), channel_id=1, source_target_pairs={{0,1},{1,0},{2,3},{3,2},{4,5},{5,4},{6,7},{7,6},{8,9},{9,8},{10,11... | collective-permute-start | bytes 393224 | tf_op jit(solution)/shard_map/ppermute | solution.py:491
  34.4 1.0 %collective-permute-done = bf16[256,2,128]{2,1,0:T(2,128)(2,1)S(1)} collective-permute-done((bf16[256,2,128]{2,1,0:T(2,128)(2,1)S(1)}, bf16[256,2,128]{2,1,0:T(2,128)(2,1)S(1)}, u32[]{:S(2)}, u32[]{:S(2)}) %collective-permute-start) | collective-permute-done | bytes 131104 | tf_op jit(solution)/shard_map/ppermute | solution.py:491
  35.3 0.3 pad_maximum_fusion
  35.6 0.0 copy-start.3
  35.6 24.0 %all_to_all.11 = bf16[256,4,128]{2,1,0:T(4,128)(2,1)S(1)} all-to-all(bf16[256,4,128]{2,1,0:T(4,128)(2,1)S(1)} %pad_maximum_fusion), channel_id=1, replica_groups={{504,506,508,510,496,498,500,502,488,490,492,494,480,482,484,486,472,47..., dimensions={0} | all-to-all | bytes 524288 | tf_op jit(solution)/shard_map/all_to_all | solution.py:495
  59.6 0.0 copy-done.3
  59.6 1.4 %shard_map.129 = f32[2,4,4,2048]{3,2,1,0:T(4,128)} custom-call(bf16[1024,128]{1,0:T(8,128)(2,1)S(1)} %bitcast.5, bf16[128,128]{1,0:T(8,128)(2,1)S(1)} %get-tuple-element.14.mix_ref, bf16[256,256]{1,0:T(8,128)(2,1)S(1)} %copy-done.3, f32[32,128]{1,0:T(8,128)S(1)} %copy-done.2), custom_call_target="tpu_custom_call" | custom-call | tf_op jit(solution)/shard_map/pallas_call | solution.py:460
Async XLA Ops:
  0.0 28.4 %copy-start = (bf16[512,256]{1,0:T(8,128)(2,1)S(1)}, bf16[512,256]{1,0:T(8,128)(2,1)}, u32[]{:S(2)}) copy-start(bf16[512,256]{1,0:T(8,128)(2,1)} %constant.19.clone.table3_ref) | copy-start | bytes 786436
  0.0 28.4 %copy-start.1 = (bf16[512,256]{1,0:T(8,128)(2,1)S(1)}, bf16[512,256]{1,0:T(8,128)(2,1)}, u32[]{:S(2)}) copy-start(bf16[512,256]{1,0:T(8,128)(2,1)} %constant.16.clone.table2_ref) | copy-start | bytes 786436
  2.4 26.0 %copy-start.2 = (f32[32,128]{1,0:T(8,128)S(1)}, f32[32,128]{1,0:T(8,128)}, u32[]{:S(2)}) copy-start(f32[32,128]{1,0:T(8,128)} %constant.15.clone.twid_hbm.twid_ref) | copy-start | bytes 49156
  2.4 26.0 %copy-start.4 = (bf16[128,128]{1,0:T(8,128)(2,1)S(1)}, bf16[128,128]{1,0:T(8,128)(2,1)}, u32[]{:S(2)}) copy-start(bf16[128,128]{1,0:T(8,128)(2,1)} %constant.17.clone.swap_ref) | copy-start | bytes 98308
  2.4 26.0 %copy-start.5 = (f32[32,128]{1,0:T(8,128)S(1)}, f32[32,128]{1,0:T(8,128)}, u32[]{:S(2)}) copy-start(f32[32,128]{1,0:T(8,128)} %constant.18.clone.mixed_ref) | copy-start | bytes 49156
  30.3 5.0 %collective-permute-start = (bf16[256,2,128]{2,1,0:T(2,128)(2,1)S(1)}, bf16[256,2,128]{2,1,0:T(2,128)(2,1)S(1)}, u32[]{:S(2)}, u32[]{:S(2)}) collective-permute-start(bf16[256,2,128]{2,1,0:T(2,128)(2,1)S(1)} %bitcast.9), channel_id=1, source_target_pairs={{0,1},{1,0},{2,3},{3,2},{4,5},{5,4},{6,7},{7,6},{8,9},{9,8},{10,11... | collective-permute-start | bytes 393224 | tf_op jit(solution)/shard_map/ppermute | solution.py:491
  35.6 24.0 %copy-start.3 = (bf16[256,256]{1,0:T(8,128)(2,1)S(1)}, bf16[256,256]{1,0:T(8,128)(2,1)}, u32[]{:S(2)}) copy-start(bf16[256,256]{1,0:T(8,128)(2,1)} %constant.20.clone.table_ref) | copy-start | bytes 393220
